TPU v7x, 8 devices: a whole 2x2x1 slice. The times are simulated.
8 devices in a mesh: dp: 1 (over z), tp: 2 (over y), ep: 4 (over x, core).
Axes of the slice: x: 2, y: 2, z: 1, core: 2. Of those that a mesh axis runs over, the one named last changes fastest.
Arguments:
- tokens: bfloat16 [1024, 2048], P(('dp', 'ep'))
- logits: float32 [1024, 8], P(('dp', 'ep'))
- w_in: bfloat16 [8, 2048, 5632], P('ep', None, 'tp')
- w_out: bfloat16 [8, 5632, 2048], P('ep', 'tp')
Outputs:
- output: bfloat16 [1024, 2048], P(('dp', 'ep'))
All inputs are finite; a program needn't handle non-finite values.
Results may differ from a plain program's by a relative error of at most 0.001.
Values are sent between devices in bfloat16 or wider.
A program may use at most 1 GiB of HBM per device.

v0:
```python
import jax
import jax.numpy as jnp
from jax import lax
from jax.sharding import PartitionSpec as P

CAP_FACTOR = 2


def solution(mesh):
    group_size = mesh.shape["ep"]

    def local_layer(tokens, logits, w_in, w_out):
        block_tokens, model_dim = tokens.shape
        experts = logits.shape[1]
        own_experts = w_in.shape[0]
        capacity = block_tokens * group_size * CAP_FACTOR // experts
        cand_max = 2 * capacity // group_size
        gate_probs = jax.nn.softmax(logits, axis=-1)
        cand_vals, cand_rows = lax.top_k(logits.T, cand_max)
        cand_tokens = tokens[cand_rows]
        recv_vals = lax.all_to_all(cand_vals.reshape(group_size, own_experts, cand_max), "ep", 0, 0)
        recv_rows = lax.all_to_all(cand_tokens.reshape(group_size, own_experts, cand_max, model_dim), "ep", 0, 0)
        merged = recv_vals.transpose(1, 0, 2).reshape(own_experts, group_size * cand_max)
        _, pick_pos = lax.top_k(merged, capacity)
        src_dev = pick_pos // cand_max
        src_slot = pick_pos % cand_max
        expert_ids = jnp.arange(own_experts)[:, None]
        picked = recv_rows[src_dev, expert_ids, src_slot]
        hidden = jax.nn.gelu(jnp.einsum("ecd,edf->ecf", picked, w_in, preferred_element_type=jnp.float32),
                             approximate=True).astype(jnp.bfloat16)
        part_out = jnp.einsum("ecf,efd->ecd", hidden, w_out, preferred_element_type=jnp.float32)
        expert_out = lax.psum(part_out, "tp").astype(jnp.bfloat16)
        back_buf = jnp.zeros((own_experts, group_size, cand_max, model_dim), jnp.bfloat16)
        back_buf = back_buf.at[expert_ids, src_dev, src_slot].set(expert_out)
        returned = lax.all_to_all(back_buf, "ep", 1, 1)
        gate_cand = gate_probs[cand_rows, jnp.arange(experts)[:, None]]
        gate_cand = gate_cand.reshape(group_size, own_experts, cand_max).transpose(1, 0, 2)
        row_ids = cand_rows.reshape(group_size, own_experts, cand_max).transpose(1, 0, 2)
        weighted = gate_cand[..., None] * returned.astype(jnp.float32)
        mix_sum = jax.ops.segment_sum(weighted.reshape(-1, model_dim), row_ids.reshape(-1),
                                      num_segments=block_tokens)
        return (tokens.astype(jnp.float32) + mix_sum).astype(jnp.bfloat16)

    row_spec = P(("dp", "ep"), None)
    return jax.shard_map(local_layer, mesh=mesh,
                         in_specs=(row_spec, row_spec, P("ep", None, "tp"), P("ep", "tp", None)),
                         out_specs=row_spec, check_vma=False)
```

profile of v0, /device:TPU:0, one launch (start us, length us, event | category | flops | bytes accessed | tf_op | source)
XLA Modules:
  0.0 382.4 jit_solution(234953238819186524)
XLA Ops:
  0.0 3.8 sort_prefixfusion
  3.8 4.6 %all-to-all-start = ((f32[4,2,128]{2,1,0:T(2,128)}), f32[4,2,128]{2,1,0:T(2,128)S(1)}, u32[]{:S(2)}, u32[]{:S(2)}) async-start(f32[4,2,128]{2,1,0:T(2,128)} %bitcast.8), calls=%async_computation | async-start | bytes 8192 | tf_op jit(solution)/shard_map/all_to_all | solution.py:21
  8.4 10.2 %gather_fusion.1 = bf16[1024,2048]{1,0:T(8,128)(2,1)} fusion(bf16[256,2048]{1,0:T(8,128)(2,1)} %param.4, s32[1024]{0:T(1024)S(1)} %bitcast_clamp_fusion), kind=kCustom, calls=%fused_computation.1 | custom fusion | bytes 8392704 | tf_op jit(solution)/shard_map/gather | solution.py:20
  18.6 0.0 all-to-all-done
  18.6 4.9 %all-to-all-start.1 = ((bf16[4,2,128,2048]{3,2,1,0:T(8,128)(2,1)}), bf16[4,2,128,2048]{3,2,1,0:T(8,128)(2,1)}, u32[]{:S(2)}, u32[]{:S(2)}) async-start(bf16[4,2,128,2048]{3,2,1,0:T(8,128)(2,1)} %bitcast.53), calls=%async_computation.1 | async-start | bytes 8388608 | tf_op jit(solution)/shard_map/all_to_all | solution.py:22
  23.5 4.0 %top_k.26 = (f32[2,512]{1,0:T(2,128)}, s32[2,512]{1,0:T(2,128)S(1)}) sort(f32[2,512]{1,0:T(2,128)S(1)} %bitcast.59, s32[2,512]{1,0:T(2,128)S(1)} %top_k.25), dimensions={1}, to_apply=%region_3.4 | sort | flops 10240 | bytes 16384 | tf_op jit(solution)/shard_map/top_k | solution.py:24
  27.6 43.8 %all-to-all-done.1 = bf16[4,2,128,2048]{3,2,1,0:T(8,128)(2,1)} async-done(((bf16[4,2,128,2048]{3,2,1,0:T(8,128)(2,1)}), bf16[4,2,128,2048]{3,2,1,0:T(8,128)(2,1)}, u32[]{:S(2)}, u32[]{:S(2)}) %all-to-all-start.1) | async-done | bytes 4194336 | tf_op jit(solution)/shard_map/all_to_all | solution.py:22
  71.4 8.7 %gather_fusion.2 = bf16[512,2048]{1,0:T(8,128)(2,1)S(1)} fusion(bf16[4,2,128,2048]{3,2,1,0:T(8,128)(2,1)} %all-to-all-done.1, s32[512]{0:T(512)S(1)} %bitcast.51), kind=kCustom, calls=%fused_computation.2 | custom fusion | bytes 4200448 | tf_op jit(solution)/shard_map/gather | solution.py:28
  80.1 21.6 %fusion.8 = f32[2,256,2048]{2,1,0:T(8,128)} fusion(bf16[2,2816,2048]{2,1,0:T(8,128)(2,1)} %param.7, bf16[2,256,2048]{2,1,0:T(8,128)(2,1)S(1)} %bitcast.55, bf16[2,2048,2816]{2,1,0:T(8,128)(2,1)} %param.6), kind=kOutput, calls=%fused_computation.15 | convolution fusion | flops 11824136192 | bytes 52428800 | tf_op jit(solution)/shard_map/ecf,efd->ecd/dot_general | solution.py:31
  101.7 101.0 %all-reduce.1 = bf16[2,256,2048]{2,1,0:T(8,128)(2,1)S(1)} all-reduce(f32[2,256,2048]{2,1,0:T(8,128)} %fusion.8), channel_id=1, replica_groups=mesh['dp'=1,'tp'=2,'ep'=4] {'tp'}, use_global_device_ids=true, to_apply=%region_4.5 | all-reduce | flops 1048576 | bytes 6291456 | tf_op jit(solution)/shard_map/psum | solution.py:32
  202.7 2.5 broadcast_in_dim.16
  205.2 96.9 %scatter_fusion = bf16[2,4,128,2048]{3,2,1,0:T(8,128)(2,1)} fusion(bf16[2,4,128,2048]{3,2,1,0:T(8,128)(2,1)} %broadcast_in_dim.16, s32[512]{0:T(512)S(1)} %bitcast.50, bf16[512,2048]{1,0:T(8,128)(2,1)S(1)} %bitcast.54), kind=kCustom, calls=%fused_computation.3 | custom fusion | bytes 6297600 | tf_op jit(solution)/shard_map/scatter | solution.py:34
  302.1 4.7 %copy.21 = bf16[2,4,128,2048]{3,2,0,1:T(8,128)(2,1)} copy(bf16[2,4,128,2048]{3,2,1,0:T(8,128)(2,1)} %scatter_fusion) | data formatting | bytes 8388608 | tf_op jit(solution)/shard_map/scatter | solution.py:34
  306.8 0.0 copy-start
  306.8 0.0 copy-start.1
  306.8 5.1 %all-to-all-start.2 = ((bf16[2,4,128,2048]{3,2,0,1:T(8,128)(2,1)}), bf16[2,4,128,2048]{3,2,0,1:T(8,128)(2,1)}, u32[]{:S(2)}, u32[]{:S(2)}) async-start(bf16[2,4,128,2048]{3,2,0,1:T(8,128)(2,1)} %copy.21), calls=%async_computation.2 | async-start | bytes 8388608 | tf_op jit(solution)/shard_map/all_to_all | solution.py:35
  311.9 0.0 copy-done
  311.9 0.2 convert_element_type.15
  312.1 0.0 copy-done.1
  312.2 6.5 %gather_fusion = f32[1024]{0:T(1024)S(1)} fusion(f32[256,8]{0,1:T(8,128)S(1)} %fusion.14, s32[1024]{0:T(1024)S(1)} %fusion.16), kind=kCustom, calls=%fused_computation | custom fusion | bytes 16384 | tf_op jit(solution)/shard_map/gather | solution.py:36
  318.8 41.0 %all-to-all-done.2 = bf16[2,4,128,2048]{3,2,0,1:T(8,128)(2,1)} async-done(((bf16[2,4,128,2048]{3,2,0,1:T(8,128)(2,1)}), bf16[2,4,128,2048]{3,2,0,1:T(8,128)(2,1)}, u32[]{:S(2)}, u32[]{:S(2)}) %all-to-all-start.2) | async-done | bytes 4194336 | tf_op jit(solution)/shard_map/all_to_all | solution.py:35
  359.8 6.0 %convert_multiply_fusion = f32[2,4,128,2048]{3,2,1,0:T(8,128)} fusion(bf16[2,4,128,2048]{3,2,0,1:T(8,128)(2,1)} %all-to-all-done.2, f32[2,4,128]{2,1,0:T(4,128)S(1)} %copy.20), kind=kLoop, calls=%fused_computation.6 | loop fusion | flops 4194304 | bytes 12587008 | tf_op jit(solution)/shard_map/mul | solution.py:39
  365.8 15.5 %scatter_fusion.1 = f32[256,2048]{1,0:T(8,128)S(1)} fusion(f32[256,2048]{1,0:T(8,128)S(1)} %convert_element_type.15, s32[1024]{0:T(1024)S(1)} %bitcast.58, f32[1024,2048]{1,0:T(8,128)} %bitcast.52), kind=kCustom, calls=%fused_computation.4 | custom fusion | flops 2097152 | bytes 25169920 | tf_op jit(solution)/shard_map/scatter-add | solution.py:40
  381.3 1.1 convert_element_type.19
  (12 shorter events, 0.1 us)
Async XLA Ops:
  3.8 14.8 %all-to-all-start = ((f32[4,2,128]{2,1,0:T(2,128)}), f32[4,2,128]{2,1,0:T(2,128)S(1)}, u32[]{:S(2)}, u32[]{:S(2)}) async-start(f32[4,2,128]{2,1,0:T(2,128)} %bitcast.8), calls=%async_computation | async-start | bytes 8192 | tf_op jit(solution)/shard_map/all_to_all | solution.py:21
  18.6 52.7 %all-to-all-start.1 = ((bf16[4,2,128,2048]{3,2,1,0:T(8,128)(2,1)}), bf16[4,2,128,2048]{3,2,1,0:T(8,128)(2,1)}, u32[]{:S(2)}, u32[]{:S(2)}) async-start(bf16[4,2,128,2048]{3,2,1,0:T(8,128)(2,1)} %bitcast.53), calls=%async_computation.1 | async-start | bytes 8388608 | tf_op jit(solution)/shard_map/all_to_all | solution.py:22
  306.8 5.1 %copy-start = (bf16[256,2048]{1,0:T(8,128)(2,1)S(1)}, bf16[256,2048]{1,0:T(8,128)(2,1)}, u32[]{:S(2)}) copy-start(bf16[256,2048]{1,0:T(8,128)(2,1)} %param.4) | copy-start | bytes 3145732
  306.8 5.3 %copy-start.1 = (f32[256,8]{0,1:T(8,128)S(1)}, f32[256,8]{0,1:T(8,128)}, u32[]{:S(2)}) copy-start(f32[256,8]{0,1:T(8,128)} %param.5) | copy-start | bytes 24580
  306.8 53.0 %all-to-all-start.2 = ((bf16[2,4,128,2048]{3,2,0,1:T(8,128)(2,1)}), bf16[2,4,128,2048]{3,2,0,1:T(8,128)(2,1)}, u32[]{:S(2)}, u32[]{:S(2)}) async-start(bf16[2,4,128,2048]{3,2,0,1:T(8,128)(2,1)} %copy.21), calls=%async_computation.2 | async-start | bytes 8388608 | tf_op jit(solution)/shard_map/all_to_all | solution.py:35
where the time goes:
time: 386 us; the launch traced here: 382 us
  local copies, waits for them, and re-layouts  130 us (34%)
  blocking collectives  101 us (26%)
  waiting for transfers between devices  84.8 us (22%)
  other arithmetic  30.7 us (8%)
  matrix products  21.6 us (6%)
  starting transfers between devices  14.5 us (4%)
    scatter x2, local copies, waits for them, and re-layouts, local_layer(): back_buf = back_buf.at[expert_ids, src_dev, src_slot].set(expert_out)  102 us
    psum x1, blocking collectives, local_layer(): expert_out = lax.psum(part_out, 'tp').astype(jnp.bfloat16)  101 us
    all_to_all x1, waiting for transfers between devices, local_layer(): lax.all_to_all(cand_tokens.reshape(group_size, own_experts, cand_max, mod...  43.8 us
    all_to_all x1, waiting for transfers between devices, local_layer(): returned = lax.all_to_all(back_buf, 'ep', 1, 1)  41 us
    dot_general x1, matrix products, local_layer(): jnp.einsum('ecf,efd->ecd', hidden, w_out, preferred_element_type=jnp.floa...  21.6 us
    scatter-add x1, other arithmetic, local_layer(): jax.ops.segment_sum(weighted.reshape(-1, model_dim), row_ids.reshape(-1),...  15.5 us
    gather x1, local copies, waits for them, and re-layouts, local_layer(): cand_tokens = tokens[cand_rows]  10.2 us
    gather x1, local copies, waits for them, and re-layouts, local_layer(): picked = recv_rows[src_dev, expert_ids, src_slot]  8.67 us
  transfers between devices with their start and end apart: 3, of which 2 were waited for; matrix products, arithmetic and copies ran while one was open for 6% of the time, Pallas kernels for 0%

commit v1 on v0

v1 whole, which is shorter than its diff:
```python
import functools

import jax
import jax.numpy as jnp
from jax import lax
from jax.experimental import pallas as pl
from jax.experimental.pallas import tpu as pltpu
from jax.sharding import PartitionSpec as P

MESH = pl.DeviceIdType.MESH
F32 = jnp.float32
BF16 = jnp.bfloat16

BLK = 256
EXPERTS = 8
OWN = 2
CAP = 256
DIM = 2048
HID = 2816
EP = 4
TOK = BLK * EP
HALF = DIM // 2
NK = 4
KC = DIM // NK
NJ = 8
NC = HALF // NJ
NB = 3
TILE = 256


def gelu(v):
    return 0.5 * v * (1.0 + jnp.tanh(v * (0.7978845608028654 + 0.035677408136300125 * (v * v))))


def column(row):
    return jnp.transpose(jnp.broadcast_to(row, (128, 128)))


def kernel(tok, lt, w_in, w_out, out,
           xall, ltall, onehot, xg, win, acc, hid, wout, snd, rcv, zall, back, gate, res,
           loc_sem, win_sem, wout_sem, out_sem,
           lt_s, lt_r, a_s, a_r, b_s, b_r, c_s, c_r, d_s, d_r, e_s, e_r,
           s_s, s_r, zc_s, zc_r, zx_s, zx_r, zf_s, zf_r, res_s, res_r):
    ep = lax.axis_index("ep")
    tp = lax.axis_index("tp")
    near = ep + 1 - 2 * lax.rem(ep, 2)
    far = lax.rem(ep + 2, 4)
    diag = 3 - ep
    peer = 1 - tp
    to_near, to_far, to_diag = {"ep": near, "tp": tp}, {"ep": far, "tp": tp}, {"ep": diag, "tp": tp}
    to_peer = {"ep": ep, "tp": peer}

    def rows(block, half=None):
        if half is None:
            return pl.ds(pl.multiple_of(block * BLK, BLK), BLK)
        return pl.ds(pl.multiple_of(block * BLK + half * (BLK // 2), BLK // 2), BLK // 2)

    def load_tok(k):
        return pltpu.make_async_copy(tok.at[:, pl.ds(k * KC, KC)], xall.at[k, rows(ep)], loc_sem.at[k])

    def load_win(e, k):
        part = pl.ds(k * KC, KC)
        return pltpu.make_async_copy(w_in.at[e, part], win.at[e, part], win_sem.at[e * NK + k])

    def load_wout(j, e, side):
        slot = lax.rem(j, NB)
        half = peer if side == 0 else tp
        cols = pl.ds(pl.multiple_of(half * HALF + j * NC, NC), NC)
        return pltpu.make_async_copy(w_out.at[e, :, cols], wout.at[slot, e, :, pl.ds(side * NC, NC)],
                                     wout_sem.at[slot, 2 * e + side])

    def remote(src, dst, send, recv, where):
        return pltpu.make_async_remote_copy(src_ref=src, dst_ref=dst, send_sem=send, recv_sem=recv,
                                            device_id=where, device_id_type=MESH)

    def moved(ref, k, r, send, recv, where):
        piece = ref.at[k, r]
        return remote(piece, piece, send.at[k], recv.at[k], where)

    def copy_lt(i, where, slot):
        return remote(lt, ltall.at[slot], lt_s.at[i], lt_r.at[i], where)

    def copy_a(k, block):
        return moved(xall, k, rows(block), a_s, a_r, to_near)

    def copy_b(k, block):
        return moved(xall, k, rows(block, tp), b_s, b_r, to_far)

    def copy_c(k, block):
        return moved(xall, k, rows(block, tp), c_s, c_r, to_near)

    def copy_d(k, half):
        return moved(xall, k, rows(far, half), d_s, d_r, to_peer)

    def copy_e(k, block):
        return moved(xall, k, rows(block, peer), e_s, e_r, to_near)

    def copy_s(j):
        return remote(snd.at[j], rcv.at[j], s_s.at[j], s_r.at[j], to_peer)

    def zrows(owner):
        return pl.ds(pl.multiple_of(owner * (OWN * CAP), OWN * CAP), OWN * CAP)

    def copy_zc(j, owner):
        return moved(zall, j, zrows(owner), zc_s, zc_r, to_near)

    def copy_zx(j, owner):
        return moved(zall, j, zrows(owner), zx_s, zx_r, to_far)

    def copy_zf(j, owner):
        return moved(zall, j, zrows(owner), zf_s, zf_r, to_near)

    def out_cols(half, j):
        return out.at[:, pl.ds(pl.multiple_of(half * HALF + j * NC, NC), NC)]

    def copy_res(j, half):
        return remote(res.at[j], out_cols(half, j), res_s.at[j], res_r.at[j], to_peer)

    def store_res(j):
        return pltpu.make_async_copy(res.at[j], out_cols(tp, j), out_sem.at[j])

    for k in range(NK):
        load_tok(k).start()
    for k in range(NK):
        for e in range(OWN):
            load_win(e, k).start()
    for j in range(NB):
        for e in range(OWN):
            for side in range(2):
                load_wout(j, e, side).start()

    barrier = pltpu.get_barrier_semaphore()
    for where in (to_near, to_far, to_diag, to_peer):
        pl.semaphore_signal(barrier, inc=1, device_id=where, device_id_type=MESH)
    pl.semaphore_wait(barrier, 4)

    for i, where in enumerate((to_near, to_far, to_diag)):
        copy_lt(i, where, ep).start()
    for k in range(NK):
        load_tok(k).wait()
        copy_b(k, ep).start()
        copy_a(k, ep).start()

    ltall[ep] = lt[...]
    for i, (where, slot) in enumerate(((to_near, near), (to_far, far), (to_diag, diag))):
        copy_lt(i, where, slot).wait_recv()

    def pick(i, _):
        expert = ep * OWN + i
        line = jnp.concatenate([ltall[b, pl.ds(expert, 1), :] for b in range(EP)], axis=1)
        rank = jnp.zeros((1, TOK), F32)
        for s in range(TOK // 128):
            col = column(line[:, s * 128:(s + 1) * 128])
            wide = jnp.concatenate([col] * (TOK // 128), axis=1)
            rank = rank + jnp.sum(jnp.where(wide > line, 1.0, 0.0), axis=0, keepdims=True)
        slots = lax.broadcasted_iota(jnp.int32, (CAP, TOK), 0).astype(F32)
        onehot[i] = jnp.where(slots == rank, 1.0, 0.0).astype(BF16)
        return 0

    lax.fori_loop(0, OWN, pick, 0)

    def first(k):
        def body(e, _):
            load_win(e, k).wait()
            xg[...] = jnp.dot(onehot[e], xall[k], preferred_element_type=F32).astype(BF16)
            for n in range(HID // TILE):
                cols = slice(n * TILE, (n + 1) * TILE)
                r = jnp.dot(xg[...], win[e, k * KC:(k + 1) * KC, cols], preferred_element_type=F32)
                if k > 0:
                    r = r + acc[e, :, cols]
                if k < NK - 1:
                    acc[e, :, cols] = r
                else:
                    hid[e, :, cols] = gelu(r).astype(BF16)
            return 0
        lax.fori_loop(0, OWN, body, 0)

    def arrive(k):
        copy_a(k, near).wait_recv()
        copy_c(k, diag).wait_recv()
        copy_e(k, diag).wait_recv()

    for k in range(NK + 2):
        if k < NK:
            copy_b(k, far).wait_recv()
            copy_c(k, far).start()
            copy_d(k, tp).start()
        if 0 <= k - 1 < NK:
            copy_d(k - 1, peer).wait_recv()
            copy_e(k - 1, far).start()
        if 0 <= k - 2 < NK:
            arrive(k - 2)
            first(k - 2)

    def second(j, _):
        slot = lax.rem(j, NB)

        def body(e, _):
            for side in range(2):
                load_wout(j, e, side).wait()
            r = jnp.dot(hid[e], wout[slot, e], preferred_element_type=F32)
            place = pl.ds(pl.multiple_of(e * CAP, CAP), CAP)
            snd[j, place, :] = r[:, :NC]
            acc[e, :, pl.ds(pl.multiple_of(j * NC, NC), NC)] = r[:, NC:]
            return 0
        lax.fori_loop(0, OWN, body, 0)
        copy_s(j).start()

        @pl.when(j + NB < NJ)
        def _():
            for e in range(OWN):
                for side in range(2):
                    load_wout(j + NB, e, side).start()
        return 0

    lax.fori_loop(0, NJ, second, 0)

    scores = lt[...]
    top = jnp.max(scores, axis=0, keepdims=True)
    grown = jnp.exp(scores - top)
    probs = grown / jnp.sum(grown, axis=0, keepdims=True)
    slots = lax.broadcasted_iota(jnp.int32, (128, CAP), 1).astype(F32)
    for e in range(EXPERTS):
        line = [ltall[b, e:e + 1, c * 128:(c + 1) * 128] for b in range(EP) for c in range(BLK // 128)]
        for c in range(BLK // 128):
            part = slice(c * 128, (c + 1) * 128)
            col = column(scores[e:e + 1, part])
            count = jnp.zeros((128, 128), F32)
            for piece in line:
                count = count + jnp.where(piece > col, 1.0, 0.0)
            rank = jnp.sum(count, axis=1, keepdims=True)
            back[e, part, :] = jnp.where(slots == rank, 1.0, 0.0).astype(BF16)
            gate[e, part, :] = column(probs[e:e + 1, part])

    def emit(j):
        copy_res(j, tp).start()
        store_res(j).start()

    for j in range(NJ + 2):
        if j < NJ:
            copy_s(j).wait_recv()
            for e in range(OWN):
                mine = acc[e, :, j * NC:(j + 1) * NC] + rcv[j, e * CAP:(e + 1) * CAP, :]
                zall[j, pl.ds(pl.multiple_of(ep * (OWN * CAP) + e * CAP, CAP), CAP), :] = mine.astype(BF16)
            copy_zx(j, ep).start()
            copy_zc(j, ep).start()
        if 0 <= j - 1 < NJ:
            copy_zx(j - 1, far).wait_recv()
            copy_zf(j - 1, far).start()
        if 0 <= j - 2 < NJ:
            copy_zc(j - 2, near).wait_recv()
            copy_zf(j - 2, diag).wait_recv()
            total = jnp.zeros((BLK, NC), F32)
            i = j - 2
            for e in range(EXPERTS):
                z = jnp.dot(back[e], zall[i, e * CAP:(e + 1) * CAP, :], preferred_element_type=F32)
                total = total + gate[e] * z
            base = i * NC
            own = xall[tp * (NK // 2) + base // KC, rows(ep), base % KC:base % KC + NC]
            res[i] = (own.astype(F32) + total).astype(BF16)
            emit(i)

    for i, where in enumerate((to_near, to_far, to_diag)):
        copy_lt(i, where, ep).wait_send()
    for k in range(NK):
        copy_a(k, ep).wait_send()
        copy_b(k, ep).wait_send()
        copy_c(k, far).wait_send()
        copy_d(k, tp).wait_send()
        copy_e(k, far).wait_send()
    for j in range(NJ):
        copy_s(j).wait_send()
        copy_zc(j, ep).wait_send()
        copy_zx(j, ep).wait_send()
        copy_zf(j, far).wait_send()
        copy_res(j, tp).wait_send()
        store_res(j).wait()
    for j in range(NJ):
        copy_res(j, peer).wait_recv()


def solution(mesh):
    def local_layer(tokens, logits, w_in, w_out):
        dma = pltpu.SemaphoreType.DMA
        scratch = [
            pltpu.VMEM((NK, TOK, KC), BF16),
            pltpu.VMEM((EP, EXPERTS, BLK), F32),
            pltpu.VMEM((OWN, CAP, TOK), BF16),
            pltpu.VMEM((CAP, KC), BF16),
            pltpu.VMEM((OWN, DIM, HID), BF16),
            pltpu.VMEM((OWN, CAP, HID), F32),
            pltpu.VMEM((OWN, CAP, HID), BF16),
            pltpu.VMEM((NB, OWN, HID, 2 * NC), BF16),
            pltpu.VMEM((NJ, OWN * CAP, NC), F32),
            pltpu.VMEM((NJ, OWN * CAP, NC), F32),
            pltpu.VMEM((NJ, EXPERTS * CAP, NC), BF16),
            pltpu.VMEM((EXPERTS, BLK, CAP), BF16),
            pltpu.VMEM((EXPERTS, BLK, NC), F32),
            pltpu.VMEM((NJ, BLK, NC), BF16),
            dma((NK,)), dma((OWN * NK,)), dma((NB, 4)), dma((NJ,)),
            dma((3,)), dma((3,)),
        ] + [dma((NK,))] * 10 + [dma((NJ,))] * 10
        return pl.pallas_call(
            kernel,
            out_shape=jax.ShapeDtypeStruct(tokens.shape, BF16),
            in_specs=[pl.BlockSpec(memory_space=pl.ANY), pl.BlockSpec(memory_space=pltpu.VMEM),
                      pl.BlockSpec(memory_space=pl.ANY), pl.BlockSpec(memory_space=pl.ANY)],
            out_specs=pl.BlockSpec(memory_space=pl.ANY),
            scratch_shapes=scratch,
            compiler_params=pltpu.CompilerParams(collective_id=0, has_side_effects=True,
                                                 vmem_limit_bytes=67_000_000),
            name="moe_layer",
        )(tokens, logits.T, w_in, w_out)

    row_spec = P(("dp", "ep"), None)
    return jax.shard_map(local_layer, mesh=mesh,
                         in_specs=(row_spec, row_spec, P("ep", None, "tp"), P("ep", "tp", None)),
                         out_specs=row_spec, check_vma=False)
```

time: 386 us -> 96.6 us (0.25)
  local copies, waits for them, and re-layouts: 130 us -> 2.3 us
  blocking collectives: 101 us -> 0 us
  Pallas kernels: 0 us -> 94.1 us
  waiting for transfers between devices: 84.8 us -> 0 us
  other arithmetic: 30.7 us -> 0 us
  matrix products: 21.6 us -> 0 us
  starting transfers between devices: 14.5 us -> 0 us
    scatter x2 -> x0, local copies, waits for them, and re-layouts: 102 us -> none  [local_layer(): back_buf = back_buf.at[expert_ids, src_dev, src_slot].set(expert_out)]
    psum x1 -> x0, blocking collectives: 101 us -> none  [local_layer(): expert_out = lax.psum(part_out, 'tp').astype(jnp.bfloat16)]
    pallas_call x0 -> x1, Pallas kernels: none -> 94.1 us  [local_layer(): pl.pallas_call(kernel, out_shape=jax.ShapeDtypeStruct(tokens.shape, BF16)...]
    all_to_all x3 -> x0, waiting for transfers between devices: 84.8 us -> none  [the longest x1 43.8 us: local_layer(): lax.all_to_all(cand_tokens.reshape(group_size, own_experts, cand_max, mod...]
    gather x3 -> x0, local copies, waits for them, and re-layouts: 25.4 us -> none  [the longest x1 10.2 us: local_layer(): cand_tokens = tokens[cand_rows]]
    dot_general x1 -> x0, matrix products: 21.6 us -> none  [local_layer(): jnp.einsum('ecf,efd->ecd', hidden, w_out, preferred_element_type=jnp.floa...]
    scatter-add x1 -> x0, other arithmetic: 15.5 us -> none  [local_layer(): jax.ops.segment_sum(weighted.reshape(-1, model_dim), row_ids.reshape(-1),...]
    all_to_all x3 -> x0, starting transfers between devices: 14.5 us -> none  [the longest x1 5.07 us: local_layer(): returned = lax.all_to_all(back_buf, 'ep', 1, 1)]
  transfers between devices with their start and end apart: 3 -> 0, of which waited for: 2 -> 0; matrix products, arithmetic and copies ran while one was open for 6% -> 0% of each run, Pallas kernels for 0% -> 0%
where the time goes in v1:
time: 96.6 us; the launch traced here: 96.4 us
  Pallas kernels  94.1 us (97%)
  local copies, waits for them, and re-layouts  2.3 us (2%)
    pallas_call x1, Pallas kernels, local_layer(): pl.pallas_call(kernel, out_shape=jax.ShapeDtypeStruct(tokens.shape, BF16)...  94.1 us
    unnamed x1, local copies, waits for them, and re-layouts  2.3 us

profile of v1, /device:TPU:0, one launch (start us, length us, event | category | flops | bytes accessed | tf_op | source)
XLA Modules:
  0.0 96.4 jit_solution(5657008825676558846)
XLA Ops:
  0.0 94.1 %moe_layer.1 = bf16[256,2048]{1,0:T(8,128)(2,1)} custom-call(bf16[256,2048]{1,0:T(8,128)(2,1)} %tok.1, f32[8,256]{1,0:T(8,128)} %bitcast.1, bf16[2,2048,2816]{2,1,0:T(8,128)(2,1)} %w_in.1, bf16[2,2816,2048]{2,1,0:T(8,128)(2,1)} %w_out.1), custom_call_target="tpu_custom_call" | custom-call | tf_op jit(solution)/shard_map/moe_layer/pallas_call | solution.py:303
  94.1 2.3 %copy.6 = bf16[256,2048]{1,0:T(8,128)(2,1)} copy(bf16[256,2048]{1,0:T(8,128)(2,1)} %moe_layer.1) | data formatting | bytes 2097152

commit v2 on v0

v2 whole, which is shorter than its diff:
```python
import jax
import jax.numpy as jnp
from jax import lax
from jax.experimental import pallas as pl
from jax.experimental.pallas import tpu as pltpu
from jax.sharding import PartitionSpec as P

MESH = pl.DeviceIdType.MESH
F32 = jnp.float32
BF16 = jnp.bfloat16

BLK = 256
HB = BLK // 2
EXPERTS = 8
OWN = 2
CAP = 256
HC = CAP // 2
DIM = 2048
HID = 2816
EP = 4
TOK = BLK * EP
HALF = DIM // 2
NQ = 4
KQ = DIM // NQ
NK = 8
KK = DIM // NK
NJ = 8
NC = HALF // NJ
NB = 3
TILE = 256
LAG = 4


def gelu(v):
    return 0.5 * v * (1.0 + jnp.tanh(v * (0.7978845608028654 + 0.035677408136300125 * (v * v))))


def column(row):
    return jnp.transpose(jnp.broadcast_to(row, (128, 128)))


def kernel(tok, lt, w_in, w_out, out,
           xall, ltall, slots, hot1, hot2, xg, win, acc, hid, wout, snd, mine, rcv, zall, back, gate, probs, res,
           loc_sem, win_sem, wout_sem, out_sem,
           lt_s, lt_r, sl_s, sl_r, a_s, a_r, b_s, b_r, c_s, c_r, d_s, d_r, e_s, e_r, f_s, f_r, g_s, g_r,
           s_s, s_r, zc_s, zc_r, zx_s, zx_r, zf_s, zf_r, res_s, res_r):
    scope = jax.named_scope
    ep = lax.axis_index("ep")
    tp = lax.axis_index("tp")
    core = lax.rem(ep, 2)
    chip = ep // 2
    near = ep + 1 - 2 * core
    far = lax.rem(ep + 2, 4)
    diag = 3 - ep
    peer = 1 - tp
    to_near, to_far, to_diag = {"ep": near, "tp": tp}, {"ep": far, "tp": tp}, {"ep": diag, "tp": tp}
    to_peer = {"ep": ep, "tp": peer}
    A, B = 2, 3
    place_near, place_far, place_diag = 1 - core, 2 + core, 3 - core

    def rows(place, half=None):
        if half is None:
            return pl.ds(pl.multiple_of(place * BLK, BLK), BLK)
        return pl.ds(pl.multiple_of(place * BLK + half * HB, HB), HB)

    def remote(src, dst, send, recv, where):
        return pltpu.make_async_remote_copy(src_ref=src, dst_ref=dst, send_sem=send, recv_sem=recv,
                                            device_id=where, device_id_type=MESH)

    def load_tok(q):
        return pltpu.make_async_copy(tok.at[:, pl.ds(q * KQ, KQ)], xall.at[q, rows(core)], loc_sem.at[q])

    def load_win(e, q):
        part = pl.ds(q * KQ, KQ)
        return pltpu.make_async_copy(w_in.at[e, part], win.at[e, part], win_sem.at[e * NQ + q])

    def load_wout(n, e, side):
        half = peer if side == 0 else tp
        cols = pl.ds(pl.multiple_of(half * HALF + (n % NJ) * NC, NC), NC)
        return pltpu.make_async_copy(w_out.at[e, :, cols], wout.at[n % NB, e, :, pl.ds(side * NC, NC)],
                                     wout_sem.at[n % NB, 2 * e + side])

    def piece(k, r):
        return xall.at[k // 2, r, pl.ds((k % 2) * KK, KK)]

    def copy_lt(i, where, place):
        return remote(lt, ltall.at[place], lt_s.at[i], lt_r.at[i], where)

    def copy_slots(i, where, place):
        return remote(slots.at[core], slots.at[place], sl_s.at[i], sl_r.at[i], where)

    def copy_a(k, place):
        return remote(piece(k, rows(place)), piece(k, rows(place)), a_s.at[k], a_r.at[k], to_near)

    def copy_b(k):
        return remote(piece(k, rows(core, tp)), piece(k, rows(A, tp)), b_s.at[k], b_r.at[k], to_far)

    def copy_c(k):
        return remote(piece(k, rows(A, tp)), piece(k, rows(A, tp)), c_s.at[k], c_r.at[k], to_near)

    def copy_d(k, half):
        return remote(piece(k, rows(A, half)), piece(k, rows(A, half)), d_s.at[k], d_r.at[k], to_peer)

    def copy_e(k):
        return remote(piece(k, rows(A, peer)), piece(k, rows(A, peer)), e_s.at[k], e_r.at[k], to_near)

    def copy_g(q):
        return remote(xall.at[q, rows(core)], xall.at[q, rows(B)], g_s.at[q], g_r.at[q], to_far)

    def copy_f(q):
        return remote(xall.at[q, rows(B)], xall.at[q, rows(B)], f_s.at[q], f_r.at[q], to_near)

    def copy_s(n):
        return remote(snd.at[n], rcv.at[n], s_s.at[n], s_r.at[n], to_peer)

    def copy_zc(n, place):
        return remote(zall.at[n, place], zall.at[n, place], zc_s.at[n], zc_r.at[n], to_near)

    def copy_zx(n, src, dst):
        return remote(zall.at[n, src], zall.at[n, dst], zx_s.at[n], zx_r.at[n], to_far)

    def copy_zf(n, place):
        return remote(zall.at[n, place], zall.at[n, place], zf_s.at[n], zf_r.at[n], to_near)

    def out_cols(half, j):
        return out.at[:, pl.ds(pl.multiple_of(half * HALF + j * NC, NC), NC)]

    def copy_res(j, half):
        return remote(res.at[j], out_cols(half, j), res_s.at[j], res_r.at[j], to_peer)

    def store_res(j):
        return pltpu.make_async_copy(res.at[j], out_cols(tp, j), out_sem.at[j])

    for q in range(NQ):
        load_tok(q).start()
    barrier = pltpu.get_barrier_semaphore()
    for where in (to_near, to_far, to_diag, to_peer):
        pl.semaphore_signal(barrier, inc=1, device_id=where, device_id_type=MESH)
    for q in range(NQ):
        load_tok(q).wait()
    for q in range(NQ):
        for e in range(OWN):
            load_win(e, q).start()
    for n in range(NB):
        for e in range(OWN):
            for side in range(2):
                load_wout(n, e, side).start()
    with scope("barrier"):
        pl.semaphore_wait(barrier, 4)

    copy_lt(0, to_near, core).start()
    copy_lt(1, to_far, 2 + core).start()
    copy_lt(2, to_diag, 2 + core).start()
    for k in range(NK):
        @pl.when(core == 0)
        def _():
            copy_b(k).start()
        copy_a(k, core).start()

    scores = lt[...]
    grown = jnp.exp(scores - jnp.max(scores, axis=0, keepdims=True))
    probs[...] = grown / jnp.sum(grown, axis=0, keepdims=True)
    ltall[core] = scores

    with scope("ltwait"):
        copy_lt(0, to_near, place_near).wait_recv()
        copy_lt(1, to_far, place_far).wait_recv()
        copy_lt(2, to_diag, place_diag).wait_recv()

    below = jnp.where(lax.broadcasted_iota(jnp.int32, (128, 128), 0) < lax.broadcasted_iota(jnp.int32, (128, 128), 1),
                      1.0, 0.0).astype(BF16)
    before = jnp.where(lax.broadcasted_iota(jnp.int32, (8, 8), 1) < lax.broadcasted_iota(jnp.int32, (8, 8), 0),
                       1.0, 0.0).astype(BF16)

    def pick(i):
        expert = ep * OWN + i
        line = jnp.concatenate([ltall[p, pl.ds(expert, 1), :] for p in range(EP)], axis=1)
        rank = jnp.zeros((1, TOK), F32)
        for s in range(TOK // 128):
            wide = jnp.concatenate([column(line[:, s * 128:(s + 1) * 128])] * (TOK // 128), axis=1)
            rank = rank + jnp.sum(jnp.where(wide > line, 1.0, 0.0), axis=0, keepdims=True)
        taken = jnp.where(rank < CAP, 1.0, 0.0)
        grid = jnp.concatenate([taken[:, s * 128:(s + 1) * 128] for s in range(8)], axis=0)
        grid16 = grid.astype(BF16)
        inside = jnp.dot(grid16, below, preferred_element_type=F32)
        ahead = jnp.sum(jnp.dot(before, grid16, preferred_element_type=F32), axis=1, keepdims=True)
        slot = jnp.where(grid > 0.5, inside + ahead, -1.0)
        slot = jnp.concatenate([slot[s:s + 1, :] for s in range(8)], axis=1)
        first_half = lax.broadcasted_iota(jnp.int32, (HC, TOK), 0).astype(F32)
        hot1[i * HC:(i + 1) * HC, :] = jnp.where(first_half[:, :3 * BLK] == slot[:, :3 * BLK], 1.0, 0.0).astype(BF16)
        hot2[i * HC:(i + 1) * HC, :] = jnp.where(first_half + HC == slot, 1.0, 0.0).astype(BF16)
        return slot

    with scope("pick"):
        slot_rows = [pick(i) for i in range(OWN)]
        slots[core] = jnp.concatenate(slot_rows + [jnp.zeros((8 - OWN, TOK), F32)], axis=0)

    def first(h, q):
        hot, depth = (hot1, 3 * BLK) if h == 0 else (hot2, TOK)
        xg[...] = jnp.dot(hot[...], xall[q, :depth, :], preferred_element_type=F32).astype(BF16)

        def body(e, _):
            if h == 0:
                load_win(e, q).wait()
            mid = pl.ds(pl.multiple_of(e * HC, HC), HC)
            for n in range(HID // TILE):
                cols = slice(n * TILE, (n + 1) * TILE)
                r = jnp.dot(xg[mid, :], win[e, q * KQ:(q + 1) * KQ, cols], preferred_element_type=F32)
                if q > 0:
                    r = r + acc[e, :, cols]
                if q < NQ - 1:
                    acc[e, :, cols] = r
                else:
                    hid[h, e, :, cols] = gelu(r).astype(BF16)
            return 0
        lax.fori_loop(0, OWN, body, 0)

    def second(h, j):
        n = h * NJ + j

        def body(e, _):
            for side in range(2):
                load_wout(n, e, side).wait()
            r = jnp.dot(hid[h, e], wout[n % NB, e], preferred_element_type=F32)
            mid = pl.ds(pl.multiple_of(e * HC, HC), HC)
            snd[n, mid, :] = r[:, :NC]
            mine[n, mid, :] = r[:, NC:]
            return 0
        lax.fori_loop(0, OWN, body, 0)
        copy_s(n).start()
        if n + NB < 2 * NJ:
            for e in range(OWN):
                for side in range(2):
                    load_wout(n + NB, e, side).start()

    def relay_d(k):
        @pl.when(core == 0)
        def _():
            copy_d(k, peer).wait_recv()
            copy_e(k).start()

    for k in range(NK):
        with scope(f"relay{k}"):
            @pl.when(core == 0)
            def _():
                copy_b(k).wait_recv()
                copy_c(k).start()
                copy_d(k, tp).start()

            @pl.when(core == 1)
            def _():
                copy_c(k).wait_recv()
                if k == NK - 2:
                    for q in range(NQ):
                        copy_g(q).start()
            if k >= LAG:
                relay_d(k - LAG)

    copy_slots(0, to_near, core).start()
    copy_slots(1, to_far, 2 + core).start()
    copy_slots(2, to_diag, 2 + core).start()

    for q in range(NQ):
        with scope(f"arrive{q}"):
            if q == 2:
                relay_d(NK - 2)
                relay_d(NK - 1)
            elif q < 2:
                relay_d(NK - LAG + q)
            for k in (2 * q, 2 * q + 1):
                copy_a(k, place_near).wait_recv()

                @pl.when(core == 1)
                def _():
                    copy_e(k).wait_recv()
        with scope(f"first{q}"):
            first(0, q)

    def relay_g(q):
        @pl.when(core == 1)
        def _():
            copy_g(q).wait_recv()
            copy_f(q).start()

    relays = {1: 0, 4: 1, 7: 2}
    for j in range(NJ):
        with scope(f"second{j}"):
            second(0, j)
        if j in relays:
            with scope(f"relayg{relays[j]}"):
                relay_g(relays[j])

    for q in range(NQ):
        with scope(f"arriveB{q}"):
            if q == 1:
                relay_g(3)

            @pl.when(core == 0)
            def _():
                copy_f(q).wait_recv()
        with scope(f"firstB{q}"):
            first(1, q)
    for j in range(NJ):
        with scope(f"secondB{j}"):
            second(1, j)

    with scope("slotwait"):
        copy_slots(0, to_near, place_near).wait_recv()
        copy_slots(1, to_far, place_far).wait_recv()
        copy_slots(2, to_diag, place_diag).wait_recv()
    with scope("back"):
        lanes = lax.broadcasted_iota(jnp.int32, (128, CAP), 1).astype(F32)
        for p in range(EP):
            mark = core if p < 2 else 2 + core
            owner = lax.rem(2 * chip + p, 4)
            for i in range(OWN):
                for c in range(BLK // 128):
                    part = slice(c * 128, (c + 1) * 128)
                    here = pl.ds(pl.multiple_of(mark * BLK + c * 128, 128), 128)
                    col = column(slots[p, i:i + 1, here])
                    back[p * OWN + i, part, :] = jnp.where(jnp.concatenate([col, col], axis=1) == lanes, 1.0, 0.0).astype(BF16)
                    gate[p * OWN + i, part, :] = column(probs[pl.ds(owner * OWN + i, 1), :][:, part])

    def close(n):
        with scope(f"waits{n}"):
            copy_s(n).wait_recv()
        zall[n, core] = (mine[n] + rcv[n]).astype(BF16)
        copy_zx(n, core, 2 + core).start()
        copy_zc(n, core).start()

    def forward(n):
        with scope(f"waitzx{n}"):
            copy_zx(n, place_far, place_far).wait_recv()
        copy_zf(n, place_far).start()

    def landed(n):
        with scope(f"waitzf{n}"):
            copy_zc(n, place_near).wait_recv()
            copy_zf(n, place_diag).wait_recv()

    def combine(j):
        total = jnp.zeros((BLK, NC), F32)
        for p in range(EP):
            for i in range(OWN):
                mid = slice(i * HC, (i + 1) * HC)
                z = jnp.concatenate([zall[j, p, mid, :], zall[NJ + j, p, mid, :]], axis=0)
                total = total + gate[p * OWN + i] * jnp.dot(back[p * OWN + i], z, preferred_element_type=F32)
        base = j * NC
        own = xall[tp * (NQ // 2) + base // KQ, rows(core), base % KQ:base % KQ + NC]
        res[j] = (own.astype(F32) + total).astype(BF16)
        copy_res(j, tp).start()
        store_res(j).start()

    for n in range(2 * NJ + 2):
        if n < 2 * NJ:
            close(n)
        if 0 <= n - 1 < 2 * NJ:
            forward(n - 1)
        if 0 <= n - 2:
            landed(n - 2)
            if n - 2 >= NJ:
                combine(n - 2 - NJ)

    with scope("drain"):
        for i, where in enumerate((to_near, to_far, to_diag)):
            copy_lt(i, where, core).wait_send()
            copy_slots(i, where, core).wait_send()
        for k in range(NK):
            copy_a(k, core).wait_send()

            @pl.when(core == 0)
            def _():
                copy_b(k).wait_send()
                copy_c(k).wait_send()
                copy_d(k, tp).wait_send()
                copy_e(k).wait_send()

        @pl.when(core == 1)
        def _():
            for q in range(NQ):
                copy_g(q).wait_send()
                copy_f(q).wait_send()
        for n in range(2 * NJ):
            copy_s(n).wait_send()
            copy_zc(n, core).wait_send()
            copy_zx(n, core, place_far).wait_send()
            copy_zf(n, place_far).wait_send()
        for j in range(NJ):
            copy_res(j, tp).wait_send()
            store_res(j).wait()
        for j in range(NJ):
            copy_res(j, peer).wait_recv()


def solution(mesh):
    def local_layer(tokens, logits, w_in, w_out):
        dma = pltpu.SemaphoreType.DMA
        scratch = [
            pltpu.VMEM((NQ, TOK, KQ), BF16),
            pltpu.VMEM((EP, EXPERTS, BLK), F32),
            pltpu.VMEM((EP, 8, TOK), F32),
            pltpu.VMEM((OWN * HC, 3 * BLK), BF16),
            pltpu.VMEM((OWN * HC, TOK), BF16),
            pltpu.VMEM((OWN * HC, KQ), BF16),
            pltpu.VMEM((OWN, DIM, HID), BF16),
            pltpu.VMEM((OWN, HC, HID), F32),
            pltpu.VMEM((2, OWN, HC, HID), BF16),
            pltpu.VMEM((NB, OWN, HID, 2 * NC), BF16),
            pltpu.VMEM((2 * NJ, OWN * HC, NC), F32),
            pltpu.VMEM((2 * NJ, OWN * HC, NC), F32),
            pltpu.VMEM((2 * NJ, OWN * HC, NC), F32),
            pltpu.VMEM((2 * NJ, EP, OWN * HC, NC), BF16),
            pltpu.VMEM((EXPERTS, BLK, CAP), BF16),
            pltpu.VMEM((EXPERTS, BLK, NC), F32),
            pltpu.VMEM((EXPERTS, BLK), F32),
            pltpu.VMEM((NJ, BLK, NC), BF16),
            dma((NQ,)), dma((OWN * NQ,)), dma((NB, 4)), dma((NJ,)),
            dma((3,)), dma((3,)), dma((3,)), dma((3,)),
        ] + [dma((NK,))] * 10 + [dma((NQ,))] * 4 + [dma((2 * NJ,))] * 8 + [dma((NJ,))] * 2
        return pl.pallas_call(
            kernel,
            out_shape=jax.ShapeDtypeStruct(tokens.shape, BF16),
            in_specs=[pl.BlockSpec(memory_space=pl.ANY), pl.BlockSpec(memory_space=pltpu.VMEM),
                      pl.BlockSpec(memory_space=pl.ANY), pl.BlockSpec(memory_space=pl.ANY)],
            out_specs=pl.BlockSpec(memory_space=pl.ANY),
            scratch_shapes=scratch,
            compiler_params=pltpu.CompilerParams(collective_id=0, has_side_effects=True,
                                                 vmem_limit_bytes=67_000_000),
            name="moe_layer",
        )(tokens, logits.T, w_in, w_out)

    row_spec = P(("dp", "ep"), None)
    return jax.shard_map(local_layer, mesh=mesh,
                         in_specs=(row_spec, row_spec, P("ep", None, "tp"), P("ep", "tp", None)),
                         out_specs=row_spec, check_vma=False)
```

time: 386 us -> 84.7 us (0.22)
  local copies, waits for them, and re-layouts: 130 us -> 2.3 us
  blocking collectives: 101 us -> 0 us
  waiting for transfers between devices: 84.8 us -> 0 us
  Pallas kernels: 0 us -> 82.1 us
  other arithmetic: 30.7 us -> 0 us
  matrix products: 21.6 us -> 0 us
  starting transfers between devices: 14.5 us -> 0 us
    scatter x2 -> x0, local copies, waits for them, and re-layouts: 102 us -> none  [local_layer(): back_buf = back_buf.at[expert_ids, src_dev, src_slot].set(expert_out)]
    psum x1 -> x0, blocking collectives: 101 us -> none  [local_layer(): expert_out = lax.psum(part_out, 'tp').astype(jnp.bfloat16)]
    all_to_all x3 -> x0, waiting for transfers between devices: 84.8 us -> none  [the longest x1 43.8 us: local_layer(): lax.all_to_all(cand_tokens.reshape(group_size, own_experts, cand_max, mod...]
    pallas_call x0 -> x1, Pallas kernels: none -> 82.1 us  [local_layer(): pl.pallas_call(kernel, out_shape=jax.ShapeDtypeStruct(tokens.shape, BF16)...]
    gather x3 -> x0, local copies, waits for them, and re-layouts: 25.4 us -> none  [the longest x1 10.2 us: local_layer(): cand_tokens = tokens[cand_rows]]
    dot_general x1 -> x0, matrix products: 21.6 us -> none  [local_layer(): jnp.einsum('ecf,efd->ecd', hidden, w_out, preferred_element_type=jnp.floa...]
    scatter-add x1 -> x0, other arithmetic: 15.5 us -> none  [local_layer(): jax.ops.segment_sum(weighted.reshape(-1, model_dim), row_ids.reshape(-1),...]
    all_to_all x3 -> x0, starting transfers between devices: 14.5 us -> none  [the longest x1 5.07 us: local_layer(): returned = lax.all_to_all(back_buf, 'ep', 1, 1)]
  transfers between devices with their start and end apart: 3 -> 0, of which waited for: 2 -> 0; matrix products, arithmetic and copies ran while one was open for 6% -> 0% of each run, Pallas kernels for 0% -> 0%
where the time goes in v2:
time: 84.7 us; the launch traced here: 84.4 us
  Pallas kernels  82.1 us (97%)
  local copies, waits for them, and re-layouts  2.3 us (3%)
    pallas_call x1, Pallas kernels, local_layer(): pl.pallas_call(kernel, out_shape=jax.ShapeDtypeStruct(tokens.shape, BF16)...  82.1 us
    unnamed x1, local copies, waits for them, and re-layouts  2.3 us

profile of v2, /device:TPU:0, one launch (start us, length us, event | category | flops | bytes accessed | tf_op | source)
XLA Modules:
  0.0 84.4 jit_solution(3038865352793619024)
XLA Ops:
  0.0 82.1 %moe_layer.1 = bf16[256,2048]{1,0:T(8,128)(2,1)} custom-call(bf16[256,2048]{1,0:T(8,128)(2,1)} %tok.1, f32[8,256]{1,0:T(8,128)} %bitcast.1, bf16[2,2048,2816]{2,1,0:T(8,128)(2,1)} %w_in.1, bf16[2,2816,2048]{2,1,0:T(8,128)(2,1)} %w_out.1), custom_call_target="tpu_custom_call" | custom-call | tf_op jit(solution)/shard_map/moe_layer/pallas_call | solution.py:420
  82.1 2.3 %copy.6 = bf16[256,2048]{1,0:T(8,128)(2,1)} copy(bf16[256,2048]{1,0:T(8,128)(2,1)} %moe_layer.1) | data formatting | bytes 2097152

commit v3 on v0

v3 whole, which is shorter than its diff:
```python
import jax
import jax.numpy as jnp
from jax import lax
from jax.experimental import pallas as pl
from jax.experimental.pallas import tpu as pltpu
from jax.sharding import PartitionSpec as P

MESH = pl.DeviceIdType.MESH
F32 = jnp.float32
BF16 = jnp.bfloat16

BLK = 256
XR = 128
YR = BLK - XR
EXPERTS = 8
OWN = 2
CAP = 256
HC = CAP // 2
DIM = 2048
HID = 2816
EP = 4
TOK = BLK * EP
HALF = DIM // 2
NK = 8
KK = DIM // NK
NG = 4
KG = DIM // NG
NJ = 8
NC = HALF // NJ
GRP = 4
NB = 6
TILE = 256
EARLY = 2


def gelu(v):
    return 0.5 * v * (1.0 + jnp.tanh(v * (0.7978845608028654 + 0.035677408136300125 * (v * v))))


def column(row):
    return jnp.transpose(jnp.broadcast_to(row, (128, 128)))


def kernel(tok, lt, w_in, w_out, out,
           xall, ltall, slots, hot1, hot2, xg, xg2, win, acc, hid, wout, snd, mine, rcv, zall, back, gate, probs, res,
           local_sem, win_sem, wout_sem, send, lt_r, sl_r, a_r, bc_r, de_r, gf_r, s_r, zx_r, zn_r, res_r):
    scope = jax.named_scope
    ep = lax.axis_index("ep")
    tp = lax.axis_index("tp")
    core = lax.rem(ep, 2)
    chip = ep // 2
    near = ep + 1 - 2 * core
    far = lax.rem(ep + 2, 4)
    diag = 3 - ep
    peer = 1 - tp
    to_near, to_far, to_diag = {"ep": near, "tp": tp}, {"ep": far, "tp": tp}, {"ep": diag, "tp": tp}
    to_peer = {"ep": ep, "tp": peer}
    A, B = 2, 3
    place_near, place_far, place_diag = 1 - core, 3 - core, 2 + core
    there = 3 - core
    lead, follow = core == 1, core == 0

    def rows(place, offset=0, size=BLK):
        return pl.ds(pl.multiple_of(place * BLK + offset, 32), size)

    def remote(src, dst, family, recv, where):
        return pltpu.make_async_remote_copy(src_ref=src, dst_ref=dst, send_sem=send.at[family], recv_sem=recv,
                                            device_id=where, device_id_type=MESH)

    def load_tok(k):
        return pltpu.make_async_copy(tok.at[:, pl.ds(k * KK, KK)], xall.at[k, rows(core)], local_sem.at[0 if k < EARLY else 1])

    def load_win(e, g):
        part = pl.ds(g * KG, KG)
        return pltpu.make_async_copy(w_in.at[e, part], win.at[e, part], win_sem.at[g])

    def wait_win(g):
        both = win.at[:, pl.ds(g * KG, KG)]
        pltpu.make_async_copy(both, both, win_sem.at[g]).wait()

    head = [(0, 0, 0), (0, 1, 0)]
    order = head + [(0, 2, 0), (0, 3, 0)] + [(0, j, 1) for j in range(4)]
    order += [(0, j, e) for j in range(4, NJ) for e in range(OWN)] + [(1, j, e) for j in range(NJ) for e in range(OWN)]

    def load_wout(m):
        if m >= len(order):
            return
        _, j, e = order[m]
        for side, half in enumerate((peer, tp)):
            cols = pl.ds(pl.multiple_of(half * HALF + j * NC, NC), NC)
            pltpu.make_async_copy(w_out.at[e, :, cols], wout.at[m % NB, :, pl.ds(side * NC, NC)], wout_sem.at[m % NB]).start()

    def wait_wout(m):
        both = wout.at[m % NB]
        pltpu.make_async_copy(both, both, wout_sem.at[m % NB]).wait()

    def copy_lt(where, place):
        return remote(ltall.at[core], ltall.at[place], 0, lt_r.at[0], where)

    def copy_slots(where, place):
        return remote(slots.at[core], slots.at[place], 1, sl_r.at[0], where)

    def copy_a(k, place):
        return remote(xall.at[k, rows(place)], xall.at[k, rows(place)], 2, a_r.at[0], to_near)

    def copy_b(k):
        return remote(xall.at[k, rows(core, tp * YR, XR)], xall.at[k, rows(A, tp * YR, XR)], 3, bc_r.at[k], to_far)

    def copy_c(k):
        piece = xall.at[k, rows(A, tp * YR, XR)]
        return remote(piece, piece, 4, bc_r.at[k], to_near)

    def copy_d(k, half):
        piece = xall.at[k, rows(A, half * XR, YR)]
        return remote(piece, piece, 5, de_r.at[k], to_peer)

    def copy_e(k):
        piece = xall.at[k, rows(A, peer * XR, YR)]
        return remote(piece, piece, 6, de_r.at[k], to_near)

    def copy_g(g):
        pair = pl.ds(2 * g, 2)
        return remote(xall.at[pair, rows(core)], xall.at[pair, rows(B)], 7, gf_r.at[g], to_far)

    def copy_f(g):
        pair = xall.at[pl.ds(2 * g, 2), rows(B)]
        return remote(pair, pair, 8, gf_r.at[g], to_near)

    def span(u):
        return (GRP * u, GRP) if u < NJ // GRP else (NJ + u - NJ // GRP, 1)

    def unit(n):
        return n // GRP if n < NJ else NJ // GRP + n - NJ

    def copy_s(n, e):
        mid = pl.ds(e * HC, HC)
        return remote(snd.at[n, mid], rcv.at[n, mid], 9, s_r.at[unit(n)], to_peer)

    def wait_s(u):
        whole = rcv.at[pl.ds(*span(u))]
        remote(whole, whole, 9, s_r.at[u], to_peer).wait_recv()

    def copy_zc(u, place):
        part = zall.at[pl.ds(*span(u)), place]
        return remote(part, part, 10, zn_r.at[max(0, u - NJ // GRP + 1)], to_near)

    def copy_zf(u, place):
        part = zall.at[pl.ds(*span(u)), place]
        return remote(part, part, 11, zn_r.at[max(0, u - NJ // GRP + 1)], to_near)

    def wait_zn(j):
        whole = zall.at[pl.ds(0, NJ), pl.ds(0, 2)] if j < 0 else zall.at[NJ + j, pl.ds(0, 2)]
        remote(whole, whole, 10, zn_r.at[j + 1], to_near).wait_recv()

    def copy_zx(u, src, dst):
        ns = pl.ds(*span(u))
        return remote(zall.at[ns, src], zall.at[ns, dst], 12, zx_r.at[u], to_far)

    def out_cols(half, j):
        return out.at[:, pl.ds(pl.multiple_of(half * HALF + j * NC, NC), NC)]

    def copy_res(j, half):
        return remote(res.at[j], out_cols(half, j), 13, res_r.at[0], to_peer)

    barrier = pltpu.get_barrier_semaphore()
    for where in (to_near, to_far, to_diag, to_peer):
        pl.semaphore_signal(barrier, inc=1, device_id=where, device_id_type=MESH)
    load_lt = pltpu.make_async_copy(lt, ltall.at[core], local_sem.at[2])
    load_lt.start()
    for k in range(NK):
        load_tok(k).start()
    mine_x = xall.at[:, rows(core)]
    load_lt.wait()
    early, late = (xall.at[pl.ds(a, n), rows(core)] for a, n in ((0, EARLY), (EARLY, NK - EARLY)))
    pltpu.make_async_copy(early, early, local_sem.at[0]).wait()
    with scope("barrier"):
        pl.semaphore_wait(barrier, 4)

    def send_pieces(ks):
        @pl.when(lead)
        def _():
            for k in ks:
                copy_b(k).start()
        for k in ks:
            copy_a(k, core).start()

    copy_lt(to_near, core).start()
    copy_lt(to_far, there).start()
    copy_lt(to_diag, there).start()
    send_pieces(range(EARLY))
    pltpu.make_async_copy(late, late, local_sem.at[1]).wait()
    send_pieces(range(EARLY, NK))
    for g in range(NG):
        for e in range(OWN):
            load_win(e, g).start()
    for m in range(NB):
        load_wout(m)

    scores = ltall[core]
    grown = jnp.exp(scores - jnp.max(scores, axis=0, keepdims=True))
    probs[...] = grown / jnp.sum(grown, axis=0, keepdims=True)

    with scope("ltwait"):
        three = ltall.at[pl.ds(0, 3)]
        remote(three, three, 0, lt_r.at[0], to_near).wait_recv()

    below = jnp.where(lax.broadcasted_iota(jnp.int32, (128, 128), 0) < lax.broadcasted_iota(jnp.int32, (128, 128), 1),
                      1.0, 0.0).astype(BF16)
    before = jnp.where(lax.broadcasted_iota(jnp.int32, (8, 8), 1) < lax.broadcasted_iota(jnp.int32, (8, 8), 0),
                       1.0, 0.0).astype(BF16)

    first_half = lax.broadcasted_iota(jnp.int32, (HC, TOK), 0).astype(F32)

    def pick(i):
        expert = ep * OWN + i
        line = jnp.concatenate([ltall[p, pl.ds(expert, 1), :] for p in range(EP)], axis=1)
        rank = jnp.zeros((1, TOK), F32)
        for s in range(TOK // 128):
            wide = jnp.concatenate([column(line[:, s * 128:(s + 1) * 128])] * (TOK // 128), axis=1)
            rank = rank + jnp.sum(jnp.where(wide > line, 1.0, 0.0), axis=0, keepdims=True)
        taken = jnp.where(rank < CAP, 1.0, 0.0)
        grid = jnp.concatenate([taken[:, s * 128:(s + 1) * 128] for s in range(8)], axis=0)
        grid16 = grid.astype(BF16)
        inside = jnp.dot(grid16, below, preferred_element_type=F32)
        ahead = jnp.sum(jnp.dot(before, grid16, preferred_element_type=F32), axis=1, keepdims=True)
        slot = jnp.where(grid > 0.5, inside + ahead, -1.0)
        slots[core, i * 8:(i + 1) * 8, :] = slot
        slot = jnp.concatenate([slot[s:s + 1, :] for s in range(8)], axis=1)
        hot1[i * HC:(i + 1) * HC, :] = jnp.where(first_half[:, :3 * BLK] == slot[:, :3 * BLK], 1.0, 0.0).astype(BF16)

    def pick_late():
        for i in range(OWN):
            slot = jnp.concatenate([slots[core, i * 8 + s:i * 8 + s + 1, :] for s in range(8)], axis=1)
            hot2[i * HC:(i + 1) * HC, :] = jnp.where(first_half + HC == slot, 1.0, 0.0).astype(BF16)

    def take_own(ks):
        for k in ks:
            xg[k] = jnp.dot(hot1[:, :2 * BLK], xall[k, :2 * BLK, :], preferred_element_type=F32).astype(BF16)

    def take_a(ks):
        for k in ks:
            r = jnp.dot(hot1[:, 2 * BLK:], xall[k, A * BLK:(A + 1) * BLK, :], preferred_element_type=F32)
            xg[k] = (xg[k].astype(F32) + r).astype(BF16)

    def first_tiles(h, g, e, x):
        for n in range(HID // TILE):
            cols = slice(n * TILE, (n + 1) * TILE)
            r = jnp.dot(x, win[e, g * KG:(g + 1) * KG, cols], preferred_element_type=F32)
            if g > 0:
                r = r + acc[e, :, cols]
            if g < NG - 1:
                acc[e, :, cols] = r
            else:
                hid[h, e, :, cols] = gelu(r).astype(BF16)

    def first(g, e):
        with scope(f"first{g}e{e}"):
            if e == 0:
                wait_win(g)
                take_a((2 * g, 2 * g + 1))
            mid = slice(e * HC, (e + 1) * HC)
            first_tiles(0, g, e, jnp.concatenate([xg[2 * g, mid, :], xg[2 * g + 1, mid, :]], axis=1))

    def first_late(g):
        for m in range(2):
            xg2[:, m * KK:(m + 1) * KK] = jnp.dot(hot2[...], xall[2 * g + m], preferred_element_type=F32).astype(BF16)

        def body(e, _):
            first_tiles(1, g, e, xg2[pl.ds(pl.multiple_of(e * HC, HC), HC), :])
            return 0
        lax.fori_loop(0, OWN, body, 0)

    def second(m):
        h, j, e = order[m]
        n = h * NJ + j
        with scope(f"second{n}e{e}"):
            wait_wout(m)
            r = jnp.dot(hid[h, e], wout[m % NB], preferred_element_type=F32)
            mid = slice(e * HC, (e + 1) * HC)
            snd[n, mid, :] = r[:, :NC]
            mine[n, mid, :] = r[:, NC:]
            copy_s(n, e).start()
            load_wout(m + NB)

    def relay_b(*ks):
        for k in ks:
            with scope(f"relayb{k}"):
                @pl.when(lead)
                def _():
                    copy_b(k).wait_recv()
                    copy_c(k).start()
                    copy_d(k, tp).start()

    def relay_d(*ks):
        for k in ks:
            with scope(f"relayd{k}"):
                @pl.when(lead)
                def _():
                    copy_d(k, peer).wait_recv()
                    copy_e(k).start()

    def ready(*ks):
        with scope(f"ready{ks[0]}"):
            @pl.when(follow)
            def _():
                for k in ks:
                    copy_c(k).wait_recv()
                    if k == NK - 2:
                        for g in range(NG):
                            copy_g(g).start()
                    copy_e(k).wait_recv()

    relay_b(0)
    with scope("pick0"):
        pick(0)
    relay_b(1)
    with scope("pick1"):
        pick(1)
    relay_b(2, 3)
    with scope("wait_a"):
        near_x = xall.at[:, rows(place_near)]
        remote(near_x, near_x, 2, a_r.at[0], to_near).wait_recv()
    with scope("own0"):
        take_own(range(4))
    relay_b(4)
    relay_d(0)
    with scope("own1"):
        take_own(range(4, NK))
    relay_b(5)
    relay_d(1)
    ready(0, 1)
    first(0, 0)
    relay_b(6)
    relay_d(2, 3)
    ready(2, 3)
    first(1, 0)
    relay_b(7)
    relay_d(4)
    first(0, 1)
    relay_d(5)
    ready(4, 5)
    first(2, 0)
    relay_d(6)
    first(1, 1)
    relay_d(7)
    ready(6, 7)
    first(3, 0)
    for m in range(len(head)):
        second(m)
    first(2, 1)
    first(3, 1)
    copy_slots(to_near, core).start()
    copy_slots(to_far, there).start()
    copy_slots(to_diag, there).start()

    def relay_g(g):
        with scope(f"relayg{g}"):
            @pl.when(follow)
            def _():
                copy_g(g).wait_recv()
                copy_f(g).start()

    half = OWN * NJ
    for m in range(len(head), half):
        second(m)
        if m in (half - 8, half - 2):
            relay_g(0 if m == half - 8 else 1)
    with scope("pick_late"):
        pick_late()
    for g in range(NG):
        if g > 0 and g + 1 < NG:
            relay_g(g + 1)
        with scope(f"readyB{g}"):
            @pl.when(lead)
            def _():
                copy_f(g).wait_recv()
        with scope(f"firstB{g}"):
            first_late(g)
    for m in range(half, 2 * half):
        second(m)

    def close(u):
        with scope(f"waits{u}"):
            wait_s(u)
        start, size = span(u)
        for n in range(start, start + size):
            zall[n, core] = (mine[n] + rcv[n]).astype(BF16)
        copy_zx(u, core, there).start()
        copy_zc(u, core).start()

    def forward(u):
        with scope(f"waitzx{u}"):
            copy_zx(u, place_far, place_far).wait_recv()
        copy_zf(u, place_far).start()

    def combine(j):
        with scope(f"waitzn{j}"):
            if j == 0:
                wait_zn(-1)
            wait_zn(j)
        total = jnp.zeros((BLK, NC), F32)
        for p in range(EP):
            for i in range(OWN):
                mid = slice(i * HC, (i + 1) * HC)
                z = jnp.concatenate([zall[j, p, mid, :], zall[NJ + j, p, mid, :]], axis=0)
                total = total + gate[p * OWN + i] * jnp.dot(back[p * OWN + i], z, preferred_element_type=F32)
        per = KK // NC
        own = xall[tp * (NK // 2) + j // per, rows(core), (j % per) * NC:(j % per + 1) * NC]
        res[j] = (own.astype(F32) + total).astype(BF16)
        copy_res(j, tp).start()
        out[:, pl.ds(pl.multiple_of(tp * HALF + j * NC, NC), NC)] = res[j]

    close(0)

    with scope("slotwait"):
        three = slots.at[pl.ds(0, 3)]
        remote(three, three, 1, sl_r.at[0], to_near).wait_recv()
    with scope("back"):
        lanes = lax.broadcasted_iota(jnp.int32, (128, CAP), 1).astype(F32)
        for p in range(EP):
            mark = core if p < 2 else there
            owner = 2 * chip + p if p < 2 else 2 * (1 - chip) + (3 - p)
            for i in range(OWN):
                for c in range(BLK // 128):
                    part = slice(c * 128, (c + 1) * 128)
                    col = column(slots[p, pl.ds(i * 8 + mark * 2 + c, 1), :])
                    back[p * OWN + i, part, :] = jnp.where(jnp.concatenate([col, col], axis=1) == lanes, 1.0, 0.0).astype(BF16)
                    gate[p * OWN + i, part, :] = column(probs[pl.ds(owner * OWN + i, 1), :][:, part])

    first_units = NJ // GRP
    units = first_units + NJ
    for u in range(1, units + 2):
        if u < units:
            close(u)
        if u - 1 < units:
            forward(u - 1)
        if u - 2 >= first_units:
            combine(u - 2 - first_units)

    with scope("drain"):
        def left(ref, family):
            remote(ref, ref, family, res_r.at[0], to_near).wait_send()
        left(ltall.at[pl.ds(0, 3)], 0)
        left(slots.at[pl.ds(0, 3)], 1)
        left(mine_x, 2)

        @pl.when(lead)
        def _():
            left(xall.at[:, rows(A, 0, XR)], 3)
            left(xall.at[:, rows(A, 0, XR)], 4)
            left(xall.at[:, rows(A, 0, YR)], 5)
            left(xall.at[:, rows(A, 0, YR)], 6)

        @pl.when(follow)
        def _():
            left(mine_x, 7)
            left(mine_x, 8)
        left(snd, 9)
        for family in (10, 11, 12):
            left(zall.at[:, 0], family)
        left(res, 13)
        remote(res, res, 13, res_r.at[0], to_peer).wait_recv()


def solution(mesh):
    def local_layer(tokens, logits, w_in, w_out):
        dma = pltpu.SemaphoreType.DMA
        units = NJ // GRP + NJ
        scratch = [
            pltpu.VMEM((NK, TOK, KK), BF16),
            pltpu.VMEM((EP, EXPERTS, BLK), F32),
            pltpu.VMEM((EP, OWN * 8, 128), F32),
            pltpu.VMEM((OWN * HC, 3 * BLK), BF16),
            pltpu.VMEM((OWN * HC, TOK), BF16),
            pltpu.VMEM((NK, OWN * HC, KK), BF16),
            pltpu.VMEM((OWN * HC, 2 * KK), BF16),
            pltpu.VMEM((OWN, DIM, HID), BF16),
            pltpu.VMEM((OWN, HC, HID), F32),
            pltpu.VMEM((2, OWN, HC, HID), BF16),
            pltpu.VMEM((NB, HID, 2 * NC), BF16),
            pltpu.VMEM((2 * NJ, OWN * HC, NC), F32),
            pltpu.VMEM((2 * NJ, OWN * HC, NC), F32),
            pltpu.VMEM((2 * NJ, OWN * HC, NC), F32),
            pltpu.VMEM((2 * NJ, EP, OWN * HC, NC), BF16),
            pltpu.VMEM((EXPERTS, BLK, CAP), BF16),
            pltpu.VMEM((EXPERTS, BLK, NC), F32),
            pltpu.VMEM((EXPERTS, BLK), F32),
            pltpu.VMEM((NJ, BLK, NC), BF16),
            dma((3,)), dma((NG,)), dma((NB,)), dma((14,)),
            dma((1,)), dma((1,)), dma((1,)), dma((NK,)), dma((NK,)), dma((NG,)),
            dma((units,)), dma((units,)), dma((1 + NJ,)), dma((1,)),
        ]
        return pl.pallas_call(
            kernel,
            out_shape=pltpu.VMEM(tokens.shape, BF16),
            in_specs=[pl.BlockSpec(memory_space=pl.ANY), pl.BlockSpec(memory_space=pl.ANY),
                      pl.BlockSpec(memory_space=pl.ANY), pl.BlockSpec(memory_space=pl.ANY)],
            out_specs=pl.BlockSpec(memory_space=pltpu.VMEM),
            scratch_shapes=scratch,
            compiler_params=pltpu.CompilerParams(collective_id=0, has_side_effects=True,
                                                 vmem_limit_bytes=62_500_000),
            name="moe_layer",
        )(tokens, logits.T, w_in, w_out)

    row_spec = P(("dp", "ep"), None)
    return jax.shard_map(local_layer, mesh=mesh,
                         in_specs=(row_spec, row_spec, P("ep", None, "tp"), P("ep", "tp", None)),
                         out_specs=row_spec, check_vma=False)
```

time: 386 us -> 76.1 us (0.20)
  local copies, waits for them, and re-layouts: 130 us -> 0.97 us
  blocking collectives: 101 us -> 0 us
  waiting for transfers between devices: 84.8 us -> 0 us
  Pallas kernels: 0 us -> 74.9 us
  other arithmetic: 30.7 us -> 0 us
  matrix products: 21.6 us -> 0 us
  starting transfers between devices: 14.5 us -> 0 us
    scatter x2 -> x0, local copies, waits for them, and re-layouts: 102 us -> none  [local_layer(): back_buf = back_buf.at[expert_ids, src_dev, src_slot].set(expert_out)]
    psum x1 -> x0, blocking collectives: 101 us -> none  [local_layer(): expert_out = lax.psum(part_out, 'tp').astype(jnp.bfloat16)]
    all_to_all x3 -> x0, waiting for transfers between devices: 84.8 us -> none  [the longest x1 43.8 us: local_layer(): lax.all_to_all(cand_tokens.reshape(group_size, own_experts, cand_max, mod...]
    pallas_call x0 -> x1, Pallas kernels: none -> 74.9 us  [local_layer(): pl.pallas_call(kernel, out_shape=pltpu.VMEM(tokens.shape, BF16), in_specs...]
    gather x3 -> x0, local copies, waits for them, and re-layouts: 25.4 us -> none  [the longest x1 10.2 us: local_layer(): cand_tokens = tokens[cand_rows]]
    dot_general x1 -> x0, matrix products: 21.6 us -> none  [local_layer(): jnp.einsum('ecf,efd->ecd', hidden, w_out, preferred_element_type=jnp.floa...]
    scatter-add x1 -> x0, other arithmetic: 15.5 us -> none  [local_layer(): jax.ops.segment_sum(weighted.reshape(-1, model_dim), row_ids.reshape(-1),...]
    all_to_all x3 -> x0, starting transfers between devices: 14.5 us -> none  [the longest x1 5.07 us: local_layer(): returned = lax.all_to_all(back_buf, 'ep', 1, 1)]
  transfers between devices with their start and end apart: 3 -> 0, of which waited for: 2 -> 0; matrix products, arithmetic and copies ran while one was open for 6% -> 0% of each run, Pallas kernels for 0% -> 0%
where the time goes in v3:
time: 76.1 us; the launch traced here: 75.9 us
  Pallas kernels  74.9 us (98%)
  local copies, waits for them, and re-layouts  0.97 us (1%)
    pallas_call x1, Pallas kernels, local_layer(): pl.pallas_call(kernel, out_shape=pltpu.VMEM(tokens.shape, BF16), in_specs...  74.9 us

profile of v3, /device:TPU:0, one launch (start us, length us, event | category | flops | bytes accessed | tf_op | source)
XLA Modules:
  0.0 75.9 jit_solution(8102031768520916659)
XLA Ops:
  0.0 74.9 %moe_layer.1 = bf16[256,2048]{1,0:T(8,128)(2,1)S(1)} custom-call(bf16[256,2048]{1,0:T(8,128)(2,1)} %tok.1, f32[8,256]{1,0:T(8,128)} %bitcast.1, bf16[2,2048,2816]{2,1,0:T(8,128)(2,1)} %w_in.1, bf16[2,2816,2048]{2,1,0:T(8,128)(2,1)} %w_out.1), custom_call_target="tpu_custom_call" | custom-call | tf_op jit(solution)/shard_map/moe_layer/pallas_call | solution.py:493
  74.9 1.0 %copy.6 = bf16[256,2048]{1,0:T(8,128)(2,1)} copy(bf16[256,2048]{1,0:T(8,128)(2,1)S(1)} %moe_layer.1) | data formatting | bytes 2097152

commit v4 on v3

v4 whole, which is shorter than its diff:
```python
import jax
import jax.numpy as jnp
from jax import lax
from jax.experimental import pallas as pl
from jax.experimental.pallas import tpu as pltpu
from jax.sharding import PartitionSpec as P

MESH = pl.DeviceIdType.MESH
F32 = jnp.float32
BF16 = jnp.bfloat16

BLK = 256
XR = 128
YR = BLK - XR
EXPERTS = 8
OWN = 2
CAP = 256
HC = CAP // 2
DIM = 2048
HID = 2816
EP = 4
TOK = BLK * EP
HALF = DIM // 2
UNIT = 128
PIECES = [(0, 1), (1, 1)] + [(u, 2) for u in range(2, 12, 2)] + [(14, 1), (12, 2), (15, 1)]
TWO_WAY = 8
NP = len(PIECES)
NG = 4
KG = DIM // NG
UG = KG // UNIT
NJ = 8
NC = HALF // NJ
SPANS = [(0, 4), (4, 4), (8, 2), (10, 2), (12, 2), (14, 1), (15, 1)]
EARLY_SPANS = 2
NB = 6
TILE = 256
EARLY = 3
EARLY_UNITS = 4


def gelu(v):
    return 0.5 * v * (1.0 + jnp.tanh(v * (0.7978845608028654 + 0.035677408136300125 * (v * v))))


def column(row):
    return jnp.transpose(jnp.broadcast_to(row, (128, 128)))


def kernel(tok, lt, w_in, w_out, out,
           xall, ltall, slots, hot1, hot2, xg, xg2, win, acc, hid, wout, snd, mine, rcv, zall, back, gate, probs, res,
           local_sem, win_sem, wout_sem, send, lt_r, sl_r, a_r, bc_r, de_r, gf_r, s_r, zx_r, zn_r, res_r):
    scope = jax.named_scope
    ep = lax.axis_index("ep")
    tp = lax.axis_index("tp")
    core = lax.rem(ep, 2)
    chip = ep // 2
    near = ep + 1 - 2 * core
    far = lax.rem(ep + 2, 4)
    diag = 3 - ep
    peer = 1 - tp
    to_near, to_far, to_diag = {"ep": near, "tp": tp}, {"ep": far, "tp": tp}, {"ep": diag, "tp": tp}
    to_peer = {"ep": ep, "tp": peer}
    A, B = 2, 3
    place_near, place_far, place_diag = 1 - core, 3 - core, 2 + core
    there = 3 - core
    lead, follow = core == 1, core == 0

    def rows(place, offset=0, size=BLK):
        return pl.ds(pl.multiple_of(place * BLK + offset, 32), size)

    def remote(src, dst, family, recv, where):
        return pltpu.make_async_remote_copy(src_ref=src, dst_ref=dst, send_sem=send.at[family], recv_sem=recv,
                                            device_id=where, device_id_type=MESH)

    def load_tok(k):
        return pltpu.make_async_copy(tok.at[:, pl.ds(k * UNIT, UNIT)], xall.at[k, rows(core)], local_sem.at[0 if k < EARLY_UNITS else 1])

    def load_win(e, g):
        part = pl.ds(g * KG, KG)
        return pltpu.make_async_copy(w_in.at[e, part], win.at[e, part], win_sem.at[OWN * g + e])

    def wait_win(e, g):
        load_win(e, g).wait()

    head = [(0, 0, 0), (0, 1, 0), (0, 2, 0)]
    order = head + [(0, 3, 0)] + [(0, j, 1) for j in range(4)]
    order += [(0, j, e) for j in range(4, NJ) for e in range(OWN)] + [(1, j, e) for j in range(NJ) for e in range(OWN)]

    def load_wout(m):
        if m >= len(order):
            return
        _, j, e = order[m]
        for side, half in enumerate((peer, tp)):
            cols = pl.ds(pl.multiple_of(half * HALF + j * NC, NC), NC)
            pltpu.make_async_copy(w_out.at[e, :, cols], wout.at[m % NB, :, pl.ds(side * NC, NC)], wout_sem.at[m % NB]).start()

    def wait_wout(m):
        both = wout.at[m % NB]
        pltpu.make_async_copy(both, both, wout_sem.at[m % NB]).wait()

    def copy_lt(where, place):
        return remote(ltall.at[core], ltall.at[place], 0, lt_r.at[0], where)

    def copy_slots(where, place):
        return remote(slots.at[core], slots.at[place], 0, sl_r.at[0], where)

    def copy_a(k, place):
        piece = xall.at[pl.ds(*PIECES[k]), rows(place)]
        return remote(piece, piece, 1, a_r.at[0], to_near)

    def b_rows(k, place):
        return rows(place, tp * YR, XR) if k < TWO_WAY else rows(place)

    def copy_b(k):
        units = pl.ds(*PIECES[k])
        return remote(xall.at[units, b_rows(k, core)], xall.at[units, b_rows(k, A)], 1, bc_r.at[k], to_far)

    def copy_c(k):
        piece = xall.at[pl.ds(*PIECES[k]), b_rows(k, A)]
        return remote(piece, piece, 1, bc_r.at[k], to_near)

    def copy_d(k, half):
        piece = xall.at[pl.ds(*PIECES[k]), rows(A, half * XR, YR)]
        return remote(piece, piece, 1, de_r.at[k], to_peer)

    def copy_e(k):
        piece = xall.at[pl.ds(*PIECES[k]), rows(A, peer * XR, YR)]
        return remote(piece, piece, 1, de_r.at[k], to_near)

    def copy_g(g):
        group = pl.ds(UG * g, UG)
        return remote(xall.at[group, rows(core)], xall.at[group, rows(B)], 1, gf_r.at[g], to_far)

    def copy_f(g):
        group = xall.at[pl.ds(UG * g, UG), rows(B)]
        return remote(group, group, 1, gf_r.at[g], to_near)

    def span(u):
        return SPANS[u]

    def unit(n):
        return [u for u, (start, size) in enumerate(SPANS) if start <= n < start + size][0]

    def copy_s(n, e):
        mid = pl.ds(e * HC, HC)
        return remote(snd.at[n, mid], rcv.at[n, mid], 3, s_r.at[unit(n)], to_peer)

    def wait_s(u):
        whole = rcv.at[pl.ds(*span(u))]
        remote(whole, whole, 3, s_r.at[u], to_peer).wait_recv()

    def copy_zc(u, place):
        part = zall.at[pl.ds(*span(u)), place]
        return remote(part, part, 2, zn_r.at[max(0, u - EARLY_SPANS + 1)], to_near)

    def copy_zf(u, place):
        part = zall.at[pl.ds(*span(u)), place]
        return remote(part, part, 2, zn_r.at[max(0, u - EARLY_SPANS + 1)], to_near)

    def wait_zn(u):
        start, size = SPANS[u] if u >= EARLY_SPANS else (0, NJ)
        whole = zall.at[pl.ds(start, size), pl.ds(0, 2)]
        remote(whole, whole, 2, zn_r.at[max(0, u - EARLY_SPANS + 1)], to_near).wait_recv()

    def copy_zx(u, src, dst):
        ns = pl.ds(*span(u))
        return remote(zall.at[ns, src], zall.at[ns, dst], 2, zx_r.at[u], to_far)

    def out_cols(half, j):
        return out.at[:, pl.ds(pl.multiple_of(half * HALF + j * NC, NC), NC)]

    def copy_res(j, half):
        return remote(res.at[j], out_cols(half, j), 3, res_r.at[0], to_peer)

    barrier = pltpu.get_barrier_semaphore()
    for where in (to_near, to_far, to_diag, to_peer):
        pl.semaphore_signal(barrier, inc=1, device_id=where, device_id_type=MESH)
    load_lt = pltpu.make_async_copy(lt, ltall.at[core], local_sem.at[2])
    load_lt.start()
    for k in range(DIM // UNIT):
        load_tok(k).start()
    mine_x = xall.at[:, rows(core)]
    load_lt.wait()
    early, late = (xall.at[pl.ds(a, n), rows(core)] for a, n in ((0, EARLY_UNITS), (EARLY_UNITS, DIM // UNIT - EARLY_UNITS)))
    pltpu.make_async_copy(early, early, local_sem.at[0]).wait()
    with scope("barrier"):
        pl.semaphore_wait(barrier, 4)

    def send_pieces(ks):
        @pl.when(lead)
        def _():
            for k in ks:
                copy_b(k).start()
        for k in ks:
            copy_a(k, core).start()

    send_pieces(range(1))
    copy_lt(to_near, core).start()
    copy_lt(to_far, there).start()
    copy_lt(to_diag, there).start()
    send_pieces(range(1, EARLY))
    pltpu.make_async_copy(late, late, local_sem.at[1]).wait()
    send_pieces(range(EARLY, NP))
    for g, e in ((0, 0), (1, 0), (0, 1), (2, 0), (3, 0), (1, 1), (2, 1), (3, 1)):
        load_win(e, g).start()

    def relay_b(*ks):
        for k in ks:
            with scope(f"relayb{k}"):
                @pl.when(lead)
                def _():
                    copy_b(k).wait_recv()
                    copy_c(k).start()
                    if k < TWO_WAY:
                        copy_d(k, tp).start()

    def relay_d(*ks):
        for k in ks:
            with scope(f"relayd{k}"):
                @pl.when(lead)
                def _():
                    copy_d(k, peer).wait_recv()
                    copy_e(k).start()

    scores = ltall[core]
    grown = jnp.exp(scores - jnp.max(scores, axis=0, keepdims=True))
    probs[...] = grown / jnp.sum(grown, axis=0, keepdims=True)

    relay_b(0, 1)
    with scope("ltwait"):
        three = ltall.at[pl.ds(0, 3)]
        remote(three, three, 0, lt_r.at[0], to_near).wait_recv()

    below = jnp.where(lax.broadcasted_iota(jnp.int32, (128, 128), 0) < lax.broadcasted_iota(jnp.int32, (128, 128), 1),
                      1.0, 0.0).astype(BF16)
    before = jnp.where(lax.broadcasted_iota(jnp.int32, (8, 8), 1) < lax.broadcasted_iota(jnp.int32, (8, 8), 0),
                       1.0, 0.0).astype(BF16)

    first_half = lax.broadcasted_iota(jnp.int32, (HC, TOK), 0).astype(F32)

    def pick(i):
        expert = ep * OWN + i
        line = jnp.concatenate([ltall[p, pl.ds(expert, 1), :] for p in range(EP)], axis=1)
        rank = jnp.zeros((1, TOK), F32)
        for s in range(TOK // 128):
            wide = jnp.concatenate([column(line[:, s * 128:(s + 1) * 128])] * (TOK // 128), axis=1)
            rank = rank + jnp.sum(jnp.where(wide > line, 1.0, 0.0), axis=0, keepdims=True)
        taken = jnp.where(rank < CAP, 1.0, 0.0)
        grid = jnp.concatenate([taken[:, s * 128:(s + 1) * 128] for s in range(8)], axis=0)
        grid16 = grid.astype(BF16)
        inside = jnp.dot(grid16, below, preferred_element_type=F32)
        ahead = jnp.sum(jnp.dot(before, grid16, preferred_element_type=F32), axis=1, keepdims=True)
        slot = jnp.where(grid > 0.5, inside + ahead, -1.0)
        slots[core, i * 8:(i + 1) * 8, :] = slot
        slot = jnp.concatenate([slot[s:s + 1, :] for s in range(8)], axis=1)
        hot1[i * HC:(i + 1) * HC, :] = jnp.where(first_half[:, :3 * BLK] == slot[:, :3 * BLK], 1.0, 0.0).astype(BF16)

    def pick_late():
        for i in range(OWN):
            slot = jnp.concatenate([slots[core, i * 8 + s:i * 8 + s + 1, :] for s in range(8)], axis=1)
            hot2[i * HC:(i + 1) * HC, :] = jnp.where(first_half + HC == slot, 1.0, 0.0).astype(BF16)

    def cut(first_unit, units, place, places):
        part = pl.ds(place * BLK, places * BLK)
        return jnp.concatenate([xall[u, part, :] for u in range(first_unit, first_unit + units)], axis=1)

    def lanes_of(first_unit, units):
        return slice(first_unit * UNIT, (first_unit + units) * UNIT)

    def take_own(pairs):
        for u in pairs:
            xg[:, lanes_of(2 * u, 2)] = jnp.dot(hot1[:, :2 * BLK], cut(2 * u, 2, 0, 2), preferred_element_type=F32).astype(BF16)

    def take_a(units):
        for u, n in units:
            cols = lanes_of(u, n)
            r = jnp.dot(hot1[:, 2 * BLK:], cut(u, n, A, 1), preferred_element_type=F32)
            xg[:, cols] = (xg[:, cols].astype(F32) + r).astype(BF16)

    def first_tiles(h, e, first_unit, units, x):
        for n in range(HID // TILE):
            cols = slice(n * TILE, (n + 1) * TILE)
            r = jnp.dot(x, win[e, first_unit * UNIT:(first_unit + units) * UNIT, cols], preferred_element_type=F32)
            if first_unit > 0:
                r = r + acc[e, :, cols]
            if first_unit + units < DIM // UNIT:
                acc[e, :, cols] = r
            else:
                hid[h, e, :, cols] = gelu(r).astype(BF16)

    def first(e, first_unit, units):
        with scope(f"first{first_unit}e{e}"):
            for g in range(NG):
                if first_unit <= g * UG < first_unit + units:
                    wait_win(e, g)
            if e == 0:
                take_a([(u, 2) for u in range(first_unit, first_unit + units, 2)])
            first_tiles(0, e, first_unit, units, xg[e * HC:(e + 1) * HC, lanes_of(first_unit, units)])

    def first_late(g):
        for m in range(0, UG, 2):
            x = cut(UG * g + m, 2, 0, EP)
            xg2[:, m * UNIT:(m + 2) * UNIT] = jnp.dot(hot2[...], x, preferred_element_type=F32).astype(BF16)

        def body(e, _):
            first_tiles(1, e, UG * g, UG, xg2[pl.ds(pl.multiple_of(e * HC, HC), HC), :])
            return 0
        lax.fori_loop(0, OWN, body, 0)

    def second(m):
        h, j, e = order[m]
        n = h * NJ + j
        with scope(f"second{n}e{e}"):
            if m > 0:
                wait_wout(m)
            mid = slice(e * HC, (e + 1) * HC)
            r = jnp.dot(hid[h, e], wout[m % NB], preferred_element_type=F32)
            snd[n, mid, :] = r[:, :NC]
            mine[n, mid, :] = r[:, NC:]
            copy_s(n, e).start()
            load_wout(m + NB)

    def ready(*ks):
        with scope(f"ready{ks[0]}"):
            @pl.when(follow)
            def _():
                for k in ks:
                    copy_c(k).wait_recv()
                    if k == NP - 1:
                        for g in range(NG):
                            copy_g(g).start()
                    if k < TWO_WAY:
                        copy_e(k).wait_recv()

    relay_b(2)
    with scope("pick0"):
        pick(0)
    relay_b(3)
    with scope("pick1"):
        pick(1)
    relay_b(4)
    with scope("wait_a"):
        near_x = xall.at[:, rows(place_near)]
        remote(near_x, near_x, 1, a_r.at[0], to_near).wait_recv()
    relay_d(0, 1)
    with scope("own0"):
        take_own(range(4))
    relay_b(5)
    with scope("own1"):
        take_own(range(4, 8))
    relay_d(2)
    relay_b(6)
    ready(0, 1, 2)
    first(0, 0, 4)
    for m in range(NB):
        load_wout(m)
    relay_b(7)
    relay_d(3, 4)
    ready(3, 4)
    first(0, 4, 4)
    relay_d(5)
    relay_b(8)
    ready(5)
    first(0, 8, 2)
    ready(8)
    first(0, 12, 2)
    relay_d(6)
    relay_b(9)
    ready(6)
    first(0, 10, 2)
    wait_wout(0)
    relay_d(7)
    ready(7, 9)
    first(0, 14, 2)
    for m in range(len(head)):
        second(m)
    first(1, 0, 4)
    first(1, 4, 4)
    first(1, 8, 4)
    first(1, 12, 4)
    copy_slots(to_near, core).start()
    copy_slots(to_far, there).start()
    copy_slots(to_diag, there).start()

    def relay_g(g):
        with scope(f"relayg{g}"):
            @pl.when(follow)
            def _():
                copy_g(g).wait_recv()
                copy_f(g).start()

    half = OWN * NJ
    for m in range(len(head), half):
        second(m)
        if m in (half - 8, half - 2):
            relay_g(0 if m == half - 8 else 1)
    with scope("pick_late"):
        pick_late()
    for g in range(NG):
        if g > 0 and g + 1 < NG:
            relay_g(g + 1)
        with scope(f"readyB{g}"):
            @pl.when(lead)
            def _():
                copy_f(g).wait_recv()
        with scope(f"firstB{g}"):
            first_late(g)
    def close(u):
        with scope(f"waits{u}"):
            wait_s(u)
        start, size = span(u)
        for n in range(start, start + size):
            zall[n, core] = (mine[n] + rcv[n]).astype(BF16)
        copy_zx(u, core, there).start()
        copy_zc(u, core).start()

    def forward(u):
        with scope(f"waitzx{u}"):
            copy_zx(u, place_far, place_far).wait_recv()
        copy_zf(u, place_far).start()

    def combine(j):
        total = jnp.zeros((BLK, NC), F32)
        for p in range(EP):
            for i in range(OWN):
                mid = slice(i * HC, (i + 1) * HC)
                z = jnp.concatenate([zall[j, p, mid, :], zall[NJ + j, p, mid, :]], axis=0)
                total = total + gate[p * OWN + i] * jnp.dot(back[p * OWN + i], z, preferred_element_type=F32)
        own = xall[tp * NJ + j, rows(core), :]
        res[j] = (own.astype(F32) + total).astype(BF16)
        copy_res(j, tp).start()
        out[:, pl.ds(pl.multiple_of(tp * HALF + j * NC, NC), NC)] = res[j]

    close(0)
    for m in range(half, 2 * half):
        second(m)


    with scope("slotwait"):
        three = slots.at[pl.ds(0, 3)]
        remote(three, three, 0, sl_r.at[0], to_near).wait_recv()
    with scope("back"):
        lanes = lax.broadcasted_iota(jnp.int32, (128, CAP), 1).astype(F32)
        for p in range(EP):
            mark = core if p < 2 else there
            owner = 2 * chip + p if p < 2 else 2 * (1 - chip) + (3 - p)
            for i in range(OWN):
                for c in range(BLK // 128):
                    part = slice(c * 128, (c + 1) * 128)
                    col = column(slots[p, pl.ds(i * 8 + mark * 2 + c, 1), :])
                    back[p * OWN + i, part, :] = jnp.where(jnp.concatenate([col, col], axis=1) == lanes, 1.0, 0.0).astype(BF16)
                    gate[p * OWN + i, part, :] = column(probs[pl.ds(owner * OWN + i, 1), :][:, part])

    units = len(SPANS)
    for u in range(1, units + 2):
        if u < units:
            close(u)
        if u - 1 < units:
            forward(u - 1)
        if u - 2 >= EARLY_SPANS:
            with scope(f"waitzn{u - 2}"):
                if u - 2 == EARLY_SPANS:
                    wait_zn(0)
                wait_zn(u - 2)
            start, size = span(u - 2)
            for n in range(start, start + size):
                combine(n - NJ)

    with scope("drain"):
        def left(ref, family):
            remote(ref, ref, family, res_r.at[0], to_near).wait_send()
        left(rcv.at[0, pl.ds(0, 96)], 0)
        left(zall.at[pl.ds(0, 12)], 1)
        left(zall.at[pl.ds(0, 12)], 2)
        left(zall.at[pl.ds(0, 10)], 3)
        remote(res, res, 3, res_r.at[0], to_peer).wait_recv()


def solution(mesh):
    def local_layer(tokens, logits, w_in, w_out):
        dma = pltpu.SemaphoreType.DMA
        units = len(SPANS)
        scratch = [
            pltpu.VMEM((DIM // UNIT, TOK, UNIT), BF16),
            pltpu.VMEM((EP, EXPERTS, BLK), F32),
            pltpu.VMEM((EP, OWN * 8, 128), F32),
            pltpu.VMEM((OWN * HC, 3 * BLK), BF16),
            pltpu.VMEM((OWN * HC, TOK), BF16),
            pltpu.VMEM((OWN * HC, DIM), BF16),
            pltpu.VMEM((OWN * HC, KG), BF16),
            pltpu.VMEM((OWN, DIM, HID), BF16),
            pltpu.VMEM((OWN, HC, HID), F32),
            pltpu.VMEM((2, OWN, HC, HID), BF16),
            pltpu.VMEM((NB, HID, 2 * NC), BF16),
            pltpu.VMEM((2 * NJ, OWN * HC, NC), F32),
            pltpu.VMEM((2 * NJ, OWN * HC, NC), F32),
            pltpu.VMEM((2 * NJ, OWN * HC, NC), F32),
            pltpu.VMEM((2 * NJ, EP, OWN * HC, NC), BF16),
            pltpu.VMEM((EXPERTS, BLK, CAP), BF16),
            pltpu.VMEM((EXPERTS, BLK, NC), F32),
            pltpu.VMEM((EXPERTS, BLK), F32),
            pltpu.VMEM((NJ, BLK, NC), BF16),
            dma((3,)), dma((OWN * NG,)), dma((NB,)), dma((4,)),
            dma((1,)), dma((1,)), dma((1,)), dma((NP,)), dma((TWO_WAY,)), dma((NG,)),
            dma((units,)), dma((units,)), dma((1 + units - EARLY_SPANS,)), dma((1,)),
        ]
        return pl.pallas_call(
            kernel,
            out_shape=pltpu.VMEM(tokens.shape, BF16),
            in_specs=[pl.BlockSpec(memory_space=pl.ANY), pl.BlockSpec(memory_space=pl.ANY),
                      pl.BlockSpec(memory_space=pl.ANY), pl.BlockSpec(memory_space=pl.ANY)],
            out_specs=pl.BlockSpec(memory_space=pltpu.VMEM),
            scratch_shapes=scratch,
            compiler_params=pltpu.CompilerParams(collective_id=0, has_side_effects=True,
                                                 vmem_limit_bytes=62_500_000),
            name="moe_layer",
        )(tokens, logits.T, w_in, w_out)

    row_spec = P(("dp", "ep"), None)
    return jax.shard_map(local_layer, mesh=mesh,
                         in_specs=(row_spec, row_spec, P("ep", None, "tp"), P("ep", "tp", None)),
                         out_specs=row_spec, check_vma=False)
```

time: 76.1 us -> 73.8 us (0.970)
  Pallas kernels: 74.9 us -> 72.7 us
    pallas_call x1, Pallas kernels: 74.9 us -> 72.7 us  [local_layer(): pl.pallas_call(kernel, out_shape=pltpu.VMEM(tokens.shape, BF16), in_specs...]
where the time goes in v4:
time: 73.8 us; the launch traced here: 73.6 us
  Pallas kernels  72.7 us (99%)
  local copies, waits for them, and re-layouts  0.97 us (1%)
    pallas_call x1, Pallas kernels, local_layer(): pl.pallas_call(kernel, out_shape=pltpu.VMEM(tokens.shape, BF16), in_specs...  72.7 us

profile of v4, /device:TPU:0, one launch (start us, length us, event | category | flops | bytes accessed | tf_op | source)
XLA Modules:
  0.0 73.6 jit_solution(13718002068588230120)
XLA Ops:
  0.0 72.7 %moe_layer.1 = bf16[256,2048]{1,0:T(8,128)(2,1)S(1)} custom-call(bf16[256,2048]{1,0:T(8,128)(2,1)} %tok.1, f32[8,256]{1,0:T(8,128)} %bitcast.1, bf16[2,2048,2816]{2,1,0:T(8,128)(2,1)} %w_in.1, bf16[2,2816,2048]{2,1,0:T(8,128)(2,1)} %w_out.1), custom_call_target="tpu_custom_call" | custom-call | tf_op jit(solution)/shard_map/moe_layer/pallas_call | solution.py:507
  72.7 1.0 %copy.6 = bf16[256,2048]{1,0:T(8,128)(2,1)} copy(bf16[256,2048]{1,0:T(8,128)(2,1)S(1)} %moe_layer.1) | data formatting | bytes 2097152

commit v5 on v4

--- a/solution.py
+++ b/solution.py
@@ -22,7 +22,7 @@
 TOK = BLK * EP
 HALF = DIM // 2
 UNIT = 128
-PIECES = [(0, 1), (1, 1)] + [(u, 2) for u in range(2, 12, 2)] + [(14, 1), (12, 2), (15, 1)]
+PIECES = [(0, 1), (1, 1), (2, 2), (4, 2), (6, 2), (8, 2), (12, 2), (14, 1), (10, 2), (15, 1)]
 TWO_WAY = 8
 NP = len(PIECES)
 NG = 4
@@ -77,10 +77,13 @@
 
     def load_win(e, g):
         part = pl.ds(g * KG, KG)
-        return pltpu.make_async_copy(w_in.at[e, part], win.at[e, part], win_sem.at[OWN * g + e])
+        return pltpu.make_async_copy(w_in.at[e, part], win.at[e, part], win_sem.at[g if e == 0 else NG])
 
     def wait_win(e, g):
-        load_win(e, g).wait()
+        if e == 0:
+            load_win(e, g).wait()
+        elif g == 0:
+            pltpu.make_async_copy(win.at[e], win.at[e], win_sem.at[NG]).wait()
 
     head = [(0, 0, 0), (0, 1, 0), (0, 2, 0)]
     order = head + [(0, 3, 0)] + [(0, j, 1) for j in range(4)]
@@ -271,13 +274,15 @@
         for u in pairs:
             xg[:, lanes_of(2 * u, 2)] = jnp.dot(hot1[:, :2 * BLK], cut(2 * u, 2, 0, 2), preferred_element_type=F32).astype(BF16)
 
-    def take_a(units):
+    def take_a(e, units):
+        mid = slice(e * HC, (e + 1) * HC)
         for u, n in units:
             cols = lanes_of(u, n)
-            r = jnp.dot(hot1[:, 2 * BLK:], cut(u, n, A, 1), preferred_element_type=F32)
-            xg[:, cols] = (xg[:, cols].astype(F32) + r).astype(BF16)
-
-    def first_tiles(h, e, first_unit, units, x):
+            r = jnp.dot(hot1[mid, 2 * BLK:], cut(u, n, A, 1), preferred_element_type=F32)
+            xg[mid, cols] = (xg[mid, cols].astype(F32) + r).astype(BF16)
+
+    def first_tiles(h, e, first_unit, units, x, w_next=None):
+        z = None
         for n in range(HID // TILE):
             cols = slice(n * TILE, (n + 1) * TILE)
             r = jnp.dot(x, win[e, first_unit * UNIT:(first_unit + units) * UNIT, cols], preferred_element_type=F32)
@@ -286,16 +291,20 @@
             if first_unit + units < DIM // UNIT:
                 acc[e, :, cols] = r
             else:
-                hid[h, e, :, cols] = gelu(r).astype(BF16)
-
-    def first(e, first_unit, units):
+                part = gelu(r).astype(BF16)
+                hid[h, e, :, cols] = part
+                if w_next is not None:
+                    step = jnp.dot(part, w_next[cols, :], preferred_element_type=F32)
+                    z = step if z is None else z + step
+        return z
+
+    def first(e, first_unit, units, w_next=None):
         with scope(f"first{first_unit}e{e}"):
             for g in range(NG):
                 if first_unit <= g * UG < first_unit + units:
                     wait_win(e, g)
-            if e == 0:
-                take_a([(u, 2) for u in range(first_unit, first_unit + units, 2)])
-            first_tiles(0, e, first_unit, units, xg[e * HC:(e + 1) * HC, lanes_of(first_unit, units)])
+            take_a(e, [(u, 2) for u in range(first_unit, first_unit + units, 2)])
+            return first_tiles(0, e, first_unit, units, xg[e * HC:(e + 1) * HC, lanes_of(first_unit, units)], w_next)
 
     def first_late(g):
         for m in range(0, UG, 2):
@@ -307,14 +316,15 @@
             return 0
         lax.fori_loop(0, OWN, body, 0)
 
-    def second(m):
+    def second(m, r=None):
         h, j, e = order[m]
         n = h * NJ + j
         with scope(f"second{n}e{e}"):
             if m > 0:
                 wait_wout(m)
             mid = slice(e * HC, (e + 1) * HC)
-            r = jnp.dot(hid[h, e], wout[m % NB], preferred_element_type=F32)
+            if r is None:
+                r = jnp.dot(hid[h, e], wout[m % NB], preferred_element_type=F32)
             snd[n, mid, :] = r[:, :NC]
             mine[n, mid, :] = r[:, NC:]
             copy_s(n, e).start()
@@ -359,20 +369,20 @@
     ready(3, 4)
     first(0, 4, 4)
     relay_d(5)
-    relay_b(8)
     ready(5)
     first(0, 8, 2)
+    relay_b(8)
     ready(8)
-    first(0, 12, 2)
+    first(0, 10, 2)
     relay_d(6)
     relay_b(9)
     ready(6)
-    first(0, 10, 2)
+    first(0, 12, 2)
     wait_wout(0)
     relay_d(7)
     ready(7, 9)
-    first(0, 14, 2)
-    for m in range(len(head)):
+    second(0, first(0, 14, 2, wout.at[0]))
+    for m in range(1, len(head)):
         second(m)
     first(1, 0, 4)
     first(1, 4, 4)
@@ -500,7 +510,7 @@
             pltpu.VMEM((EXPERTS, BLK, NC), F32),
             pltpu.VMEM((EXPERTS, BLK), F32),
             pltpu.VMEM((NJ, BLK, NC), BF16),
-            dma((3,)), dma((OWN * NG,)), dma((NB,)), dma((4,)),
+            dma((3,)), dma((NG + 1,)), dma((NB,)), dma((4,)),
             dma((1,)), dma((1,)), dma((1,)), dma((NP,)), dma((TWO_WAY,)), dma((NG,)),
             dma((units,)), dma((units,)), dma((1 + units - EARLY_SPANS,)), dma((1,)),
         ]

time: 73.8 us -> 73.5 us (level)
  no operation moved by 1% of the time
where the time goes in v5:
time: 73.5 us; the launch traced here: 73.4 us
  Pallas kernels  72.4 us (99%)
  local copies, waits for them, and re-layouts  0.97 us (1%)
    pallas_call x1, Pallas kernels, local_layer(): pl.pallas_call(kernel, out_shape=pltpu.VMEM(tokens.shape, BF16), in_specs...  72.4 us

profile of v5, /device:TPU:0, one launch (start us, length us, event | category | flops | bytes accessed | tf_op | source)
XLA Modules:
  0.0 73.4 jit_solution(6707036576793943764)
XLA Ops:
  0.0 72.4 %moe_layer.1 = bf16[256,2048]{1,0:T(8,128)(2,1)S(1)} custom-call(bf16[256,2048]{1,0:T(8,128)(2,1)} %tok.1, f32[8,256]{1,0:T(8,128)} %bitcast.1, bf16[2,2048,2816]{2,1,0:T(8,128)(2,1)} %w_in.1, bf16[2,2816,2048]{2,1,0:T(8,128)(2,1)} %w_out.1), custom_call_target="tpu_custom_call" | custom-call | tf_op jit(solution)/shard_map/moe_layer/pallas_call | solution.py:517
  72.4 1.0 %copy.6 = bf16[256,2048]{1,0:T(8,128)(2,1)} copy(bf16[256,2048]{1,0:T(8,128)(2,1)S(1)} %moe_layer.1) | data formatting | bytes 2097152

commit v6 on v5

--- a/solution.py
+++ b/solution.py
@@ -47,7 +47,7 @@
 
 
 def kernel(tok, lt, w_in, w_out, out,
-           xall, ltall, slots, hot1, hot2, xg, xg2, win, acc, hid, wout, snd, mine, rcv, zall, back, gate, probs, res,
+           xall, score, ltsend, ltall, slots, hot1, hot2, xg, xg2, win, acc, hid, wout, snd, mine, rcv, zall, back, gate, probs, res,
            local_sem, win_sem, wout_sem, send, lt_r, sl_r, a_r, bc_r, de_r, gf_r, s_r, zx_r, zn_r, res_r):
     scope = jax.named_scope
     ep = lax.axis_index("ep")
@@ -85,8 +85,8 @@
         elif g == 0:
             pltpu.make_async_copy(win.at[e], win.at[e], win_sem.at[NG]).wait()
 
-    head = [(0, 0, 0), (0, 1, 0), (0, 2, 0)]
-    order = head + [(0, 3, 0)] + [(0, j, 1) for j in range(4)]
+    head = [(0, j, 0) for j in range(4)]
+    order = head + [(0, j, 1) for j in range(4)]
     order += [(0, j, e) for j in range(4, NJ) for e in range(OWN)] + [(1, j, e) for j in range(NJ) for e in range(OWN)]
 
     def load_wout(m):
@@ -101,8 +101,8 @@
         both = wout.at[m % NB]
         pltpu.make_async_copy(both, both, wout_sem.at[m % NB]).wait()
 
-    def copy_lt(where, place):
-        return remote(ltall.at[core], ltall.at[place], 0, lt_r.at[0], where)
+    def copy_lt(where, target, place):
+        return remote(ltsend.at[target], ltall.at[place], 4, lt_r.at[0], where)
 
     def copy_slots(where, place):
         return remote(slots.at[core], slots.at[place], 0, sl_r.at[0], where)
@@ -178,12 +178,14 @@
     barrier = pltpu.get_barrier_semaphore()
     for where in (to_near, to_far, to_diag, to_peer):
         pl.semaphore_signal(barrier, inc=1, device_id=where, device_id_type=MESH)
-    load_lt = pltpu.make_async_copy(lt, ltall.at[core], local_sem.at[2])
+    load_lt = pltpu.make_async_copy(lt, score, local_sem.at[2])
     load_lt.start()
     for k in range(DIM // UNIT):
         load_tok(k).start()
     mine_x = xall.at[:, rows(core)]
     load_lt.wait()
+    for d in range(EP):
+        ltsend[d] = score[d * OWN:(d + 1) * OWN, :]
     early, late = (xall.at[pl.ds(a, n), rows(core)] for a, n in ((0, EARLY_UNITS), (EARLY_UNITS, DIM // UNIT - EARLY_UNITS)))
     pltpu.make_async_copy(early, early, local_sem.at[0]).wait()
     with scope("barrier"):
@@ -198,9 +200,9 @@
             copy_a(k, core).start()
 
     send_pieces(range(1))
-    copy_lt(to_near, core).start()
-    copy_lt(to_far, there).start()
-    copy_lt(to_diag, there).start()
+    copy_lt(to_near, near, core).start()
+    copy_lt(to_far, far, there).start()
+    copy_lt(to_diag, diag, there).start()
     send_pieces(range(1, EARLY))
     pltpu.make_async_copy(late, late, local_sem.at[1]).wait()
     send_pieces(range(EARLY, NP))
@@ -225,14 +227,15 @@
                     copy_d(k, peer).wait_recv()
                     copy_e(k).start()
 
-    scores = ltall[core]
+    scores = score[...]
+    ltall[core] = ltsend[ep]
     grown = jnp.exp(scores - jnp.max(scores, axis=0, keepdims=True))
     probs[...] = grown / jnp.sum(grown, axis=0, keepdims=True)
 
     relay_b(0, 1)
     with scope("ltwait"):
         three = ltall.at[pl.ds(0, 3)]
-        remote(three, three, 0, lt_r.at[0], to_near).wait_recv()
+        remote(three, three, 4, lt_r.at[0], to_near).wait_recv()
 
     below = jnp.where(lax.broadcasted_iota(jnp.int32, (128, 128), 0) < lax.broadcasted_iota(jnp.int32, (128, 128), 1),
                       1.0, 0.0).astype(BF16)
@@ -242,8 +245,7 @@
     first_half = lax.broadcasted_iota(jnp.int32, (HC, TOK), 0).astype(F32)
 
     def pick(i):
-        expert = ep * OWN + i
-        line = jnp.concatenate([ltall[p, pl.ds(expert, 1), :] for p in range(EP)], axis=1)
+        line = jnp.concatenate([ltall[p, i:i + 1, :] for p in range(EP)], axis=1)
         rank = jnp.zeros((1, TOK), F32)
         for s in range(TOK // 128):
             wide = jnp.concatenate([column(line[:, s * 128:(s + 1) * 128])] * (TOK // 128), axis=1)
@@ -375,10 +377,10 @@
     ready(8)
     first(0, 10, 2)
     relay_d(6)
-    relay_b(9)
     ready(6)
     first(0, 12, 2)
     wait_wout(0)
+    relay_b(9)
     relay_d(7)
     ready(7, 9)
     second(0, first(0, 14, 2, wout.at[0]))
@@ -479,7 +481,8 @@
     with scope("drain"):
         def left(ref, family):
             remote(ref, ref, family, res_r.at[0], to_near).wait_send()
-        left(rcv.at[0, pl.ds(0, 96)], 0)
+        left(ltall.at[pl.ds(0, 3)], 4)
+        left(slots.at[pl.ds(0, 3)], 0)
         left(zall.at[pl.ds(0, 12)], 1)
         left(zall.at[pl.ds(0, 12)], 2)
         left(zall.at[pl.ds(0, 10)], 3)
@@ -492,7 +495,9 @@
         units = len(SPANS)
         scratch = [
             pltpu.VMEM((DIM // UNIT, TOK, UNIT), BF16),
-            pltpu.VMEM((EP, EXPERTS, BLK), F32),
+            pltpu.VMEM((EXPERTS, BLK), F32),
+            pltpu.VMEM((EP, OWN, BLK), F32),
+            pltpu.VMEM((EP, OWN, BLK), F32),
             pltpu.VMEM((EP, OWN * 8, 128), F32),
             pltpu.VMEM((OWN * HC, 3 * BLK), BF16),
             pltpu.VMEM((OWN * HC, TOK), BF16),
@@ -510,7 +515,7 @@
             pltpu.VMEM((EXPERTS, BLK, NC), F32),
             pltpu.VMEM((EXPERTS, BLK), F32),
             pltpu.VMEM((NJ, BLK, NC), BF16),
-            dma((3,)), dma((NG + 1,)), dma((NB,)), dma((4,)),
+            dma((3,)), dma((NG + 1,)), dma((NB,)), dma((5,)),
             dma((1,)), dma((1,)), dma((1,)), dma((NP,)), dma((TWO_WAY,)), dma((NG,)),
             dma((units,)), dma((units,)), dma((1 + units - EARLY_SPANS,)), dma((1,)),
         ]

time: 73.5 us -> 73.2 us (level)
  no operation moved by 1% of the time
where the time goes in v6:
time: 73.2 us; the launch traced here: 73 us
  Pallas kernels  72.1 us (98%)
  local copies, waits for them, and re-layouts  0.97 us (1%)
    pallas_call x1, Pallas kernels, local_layer(): pl.pallas_call(kernel, out_shape=pltpu.VMEM(tokens.shape, BF16), in_specs...  72.1 us

profile of v6, /device:TPU:0, one launch (start us, length us, event | category | flops | bytes accessed | tf_op | source)
XLA Modules:
  0.0 73.0 jit_solution(9995530608678307591)
XLA Ops:
  0.0 72.1 %moe_layer.1 = bf16[256,2048]{1,0:T(8,128)(2,1)S(1)} custom-call(bf16[256,2048]{1,0:T(8,128)(2,1)} %tok.1, f32[8,256]{1,0:T(8,128)} %bitcast.1, bf16[2,2048,2816]{2,1,0:T(8,128)(2,1)} %w_in.1, bf16[2,2816,2048]{2,1,0:T(8,128)(2,1)} %w_out.1), custom_call_target="tpu_custom_call" | custom-call | tf_op jit(solution)/shard_map/moe_layer/pallas_call | solution.py:522
  72.1 1.0 %copy.6 = bf16[256,2048]{1,0:T(8,128)(2,1)} copy(bf16[256,2048]{1,0:T(8,128)(2,1)S(1)} %moe_layer.1) | data formatting | bytes 2097152

commit v7 on v6

--- a/solution.py
+++ b/solution.py
@@ -47,8 +47,8 @@
 
 
 def kernel(tok, lt, w_in, w_out, out,
-           xall, score, ltsend, ltall, slots, hot1, hot2, xg, xg2, win, acc, hid, wout, snd, mine, rcv, zall, back, gate, probs, res,
-           local_sem, win_sem, wout_sem, send, lt_r, sl_r, a_r, bc_r, de_r, gf_r, s_r, zx_r, zn_r, res_r):
+           xall, score, ltsend, ltall, slots, hot1, hot2, xg, xg2, win, acc, hid, wout, snd, mine, rcv, zall, back, gate, probs, res, passed,
+           local_sem, win_sem, wout_sem, send, lt_r, sl_r, a_r, bc_r, de_r, gf_r, s_r, zx_r, zn_r, res_r, pass_r):
     scope = jax.named_scope
     ep = lax.axis_index("ep")
     tp = lax.axis_index("tp")
@@ -60,6 +60,7 @@
     peer = 1 - tp
     to_near, to_far, to_diag = {"ep": near, "tp": tp}, {"ep": far, "tp": tp}, {"ep": diag, "tp": tp}
     to_peer = {"ep": ep, "tp": peer}
+    to_near_peer = {"ep": near, "tp": peer}
     A, B = 2, 3
     place_near, place_far, place_diag = 1 - core, 3 - core, 2 + core
     there = 3 - core
@@ -77,13 +78,16 @@
 
     def load_win(e, g):
         part = pl.ds(g * KG, KG)
-        return pltpu.make_async_copy(w_in.at[e, part], win.at[e, part], win_sem.at[g if e == 0 else NG])
+        return pltpu.make_async_copy(w_in.at[e, part], win.at[e, part], win_sem.at[min(g, 1) if e == 0 else 2])
 
     def wait_win(e, g):
-        if e == 0:
+        if e == 0 and g == 0:
             load_win(e, g).wait()
+        elif e == 0 and g == 1:
+            rest = win.at[e, pl.ds(KG, DIM - KG)]
+            pltpu.make_async_copy(rest, rest, win_sem.at[1]).wait()
         elif g == 0:
-            pltpu.make_async_copy(win.at[e], win.at[e], win_sem.at[NG]).wait()
+            pltpu.make_async_copy(win.at[e], win.at[e], win_sem.at[2]).wait()
 
     head = [(0, j, 0) for j in range(4)]
     order = head + [(0, j, 1) for j in range(4)]
@@ -174,6 +178,12 @@
 
     def copy_res(j, half):
         return remote(res.at[j], out_cols(half, j), 3, res_r.at[0], to_peer)
+
+    def copy_pass():
+        return remote(res.at[0], passed, 3, pass_r.at[0], to_near)
+
+    def copy_passed():
+        return remote(passed, out_cols(tp, 0), 5, res_r.at[0], to_near_peer)
 
     barrier = pltpu.get_barrier_semaphore()
     for where in (to_near, to_far, to_diag, to_peer):
@@ -206,8 +216,9 @@
     send_pieces(range(1, EARLY))
     pltpu.make_async_copy(late, late, local_sem.at[1]).wait()
     send_pieces(range(EARLY, NP))
-    for g, e in ((0, 0), (1, 0), (0, 1), (2, 0), (3, 0), (1, 1), (2, 1), (3, 1)):
-        load_win(e, g).start()
+    for e in range(OWN):
+        for g in range(NG):
+            load_win(e, g).start()
 
     def relay_b(*ks):
         for k in ks:
@@ -440,7 +451,16 @@
                 total = total + gate[p * OWN + i] * jnp.dot(back[p * OWN + i], z, preferred_element_type=F32)
         own = xall[tp * NJ + j, rows(core), :]
         res[j] = (own.astype(F32) + total).astype(BF16)
-        copy_res(j, tp).start()
+        if j > 0:
+            copy_res(j, tp).start()
+        else:
+            @pl.when(lead)
+            def _():
+                copy_res(j, tp).start()
+
+            @pl.when(follow)
+            def _():
+                copy_pass().start()
         out[:, pl.ds(pl.multiple_of(tp * HALF + j * NC, NC), NC)] = res[j]
 
     close(0)
@@ -477,6 +497,11 @@
             start, size = span(u - 2)
             for n in range(start, start + size):
                 combine(n - NJ)
+            if u - 2 == EARLY_SPANS + 1:
+                @pl.when(lead)
+                def _():
+                    copy_pass().wait_recv()
+                    copy_passed().start()
 
     with scope("drain"):
         def left(ref, family):
@@ -486,6 +511,10 @@
         left(zall.at[pl.ds(0, 12)], 1)
         left(zall.at[pl.ds(0, 12)], 2)
         left(zall.at[pl.ds(0, 10)], 3)
+
+        @pl.when(lead)
+        def _():
+            left(passed, 5)
         remote(res, res, 3, res_r.at[0], to_peer).wait_recv()
 
 
@@ -515,9 +544,10 @@
             pltpu.VMEM((EXPERTS, BLK, NC), F32),
             pltpu.VMEM((EXPERTS, BLK), F32),
             pltpu.VMEM((NJ, BLK, NC), BF16),
-            dma((3,)), dma((NG + 1,)), dma((NB,)), dma((5,)),
+            pltpu.VMEM((BLK, NC), BF16),
+            dma((3,)), dma((3,)), dma((NB,)), dma((6,)),
             dma((1,)), dma((1,)), dma((1,)), dma((NP,)), dma((TWO_WAY,)), dma((NG,)),
-            dma((units,)), dma((units,)), dma((1 + units - EARLY_SPANS,)), dma((1,)),
+            dma((units,)), dma((units,)), dma((1 + units - EARLY_SPANS,)), dma((1,)), dma((1,)),
         ]
         return pl.pallas_call(
             kernel,

time: 73.2 us -> 73.2 us (level)
  no operation moved by 1% of the time
where the time goes in v7:
time: 73.2 us; the launch traced here: 73 us
  Pallas kernels  72.1 us (98%)
  local copies, waits for them, and re-layouts  0.97 us (1%)
    pallas_call x1, Pallas kernels, local_layer(): pl.pallas_call(kernel, out_shape=pltpu.VMEM(tokens.shape, BF16), in_specs...  72.1 us

profile of v7, /device:TPU:0, one launch (start us, length us, event | category | flops | bytes accessed | tf_op | source)
XLA Modules:
  0.0 73.0 jit_solution(4135974254187347624)
XLA Ops:
  0.0 72.1 %moe_layer.1 = bf16[256,2048]{1,0:T(8,128)(2,1)S(1)} custom-call(bf16[256,2048]{1,0:T(8,128)(2,1)} %tok.1, f32[8,256]{1,0:T(8,128)} %bitcast.1, bf16[2,2048,2816]{2,1,0:T(8,128)(2,1)} %w_in.1, bf16[2,2816,2048]{2,1,0:T(8,128)(2,1)} %w_out.1), custom_call_target="tpu_custom_call" | custom-call | tf_op jit(solution)/shard_map/moe_layer/pallas_call | solution.py:552
  72.1 1.0 %copy.6 = bf16[256,2048]{1,0:T(8,128)(2,1)} copy(bf16[256,2048]{1,0:T(8,128)(2,1)S(1)} %moe_layer.1) | data formatting | bytes 2097152

commit v8 on v7

--- a/solution.py
+++ b/solution.py
@@ -487,8 +487,6 @@
     for u in range(1, units + 2):
         if u < units:
             close(u)
-        if u - 1 < units:
-            forward(u - 1)
         if u - 2 >= EARLY_SPANS:
             with scope(f"waitzn{u - 2}"):
                 if u - 2 == EARLY_SPANS:
@@ -502,6 +500,8 @@
                 def _():
                     copy_pass().wait_recv()
                     copy_passed().start()
+        if u - 1 < units:
+            forward(u - 1)
 
     with scope("drain"):
         def left(ref, family):

time: 73.2 us -> 73 us (level)
  no operation moved by 1% of the time
where the time goes in v8:
time: 73 us; the launch traced here: 72.9 us
  Pallas kernels  71.9 us (98%)
  local copies, waits for them, and re-layouts  0.97 us (1%)
    pallas_call x1, Pallas kernels, local_layer(): pl.pallas_call(kernel, out_shape=pltpu.VMEM(tokens.shape, BF16), in_specs...  71.9 us

profile of v8, /device:TPU:0, one launch (start us, length us, event | category | flops | bytes accessed | tf_op | source)
XLA Modules:
  0.0 72.9 jit_solution(12541767165157386771)
XLA Ops:
  0.0 71.9 %moe_layer.1 = bf16[256,2048]{1,0:T(8,128)(2,1)S(1)} custom-call(bf16[256,2048]{1,0:T(8,128)(2,1)} %tok.1, f32[8,256]{1,0:T(8,128)} %bitcast.1, bf16[2,2048,2816]{2,1,0:T(8,128)(2,1)} %w_in.1, bf16[2,2816,2048]{2,1,0:T(8,128)(2,1)} %w_out.1), custom_call_target="tpu_custom_call" | custom-call | tf_op jit(solution)/shard_map/moe_layer/pallas_call | solution.py:552
  71.9 1.0 %copy.6 = bf16[256,2048]{1,0:T(8,128)(2,1)} copy(bf16[256,2048]{1,0:T(8,128)(2,1)S(1)} %moe_layer.1) | data formatting | bytes 2097152
